TPU v7x, 8 devices: a whole 2x2x1 slice. The times are simulated.
8 devices in a mesh: part: 1 (over z), data: 2 (over y), seq: 4 (over x, core).
Axes of the slice: x: 2, y: 2, z: 1, core: 2. Of those that a mesh axis runs over, the one named last changes fastest.
Arguments:
- enc_out: bfloat16 [32, 96, 1024], P(('part', 'data'), 'seq')
- pred_out: bfloat16 [32, 24, 1024], P(('part', 'data'))
- w_enc: bfloat16 [1024, 640], replicated
- w_pred: bfloat16 [1024, 640], replicated
- w_out: bfloat16 [640, 1024], replicated
- labels: int32 [32, 23], P(('part', 'data'))
- frame_len: int32 [32], P(('part', 'data'))
- label_len: int32 [32], P(('part', 'data'))
Outputs:
- output 1: float32 [32], P(('part', 'data'))
- output 2: bfloat16 [32, 96, 1024], P(('part', 'data'), 'seq')
- output 3: float32 [32, 24, 1024], P(('part', 'data'))
- output 4: float32 [1024, 640], P('part')
- output 5: float32 [1024, 640], P('part')
- output 6: float32 [640, 1024], P('part')
All inputs are finite; a program needn't handle non-finite values.
Results may differ from a plain program's by a relative error of at most 0.013132.
Values are sent between devices in bfloat16 or wider.
A program may use at most 1 GiB of HBM per device.

v0:
```python
import jax
import jax.numpy as jnp
from jax import lax
from jax.sharding import PartitionSpec as P

NEG_FILL = -1e30


def joint_forward(enc_loc, pred_loc, w_enc, w_pred, w_out, lab_ids):
    act_enc = jnp.einsum("bth,hj->btj", enc_loc, w_enc, preferred_element_type=jnp.float32).astype(jnp.bfloat16)
    act_pred = jnp.einsum("buh,hj->buj", pred_loc, w_pred, preferred_element_type=jnp.float32).astype(jnp.bfloat16)
    hidden = jnp.tanh(act_enc.astype(jnp.float32)[:, :, None, :] + act_pred.astype(jnp.float32)[:, None, :, :]).astype(jnp.bfloat16)
    logits = jnp.einsum("btuj,jv->btuv", hidden, w_out, preferred_element_type=jnp.float32)
    log_norm = jax.nn.logsumexp(logits, axis=-1)
    w_label = jnp.take(w_out, lab_ids, axis=1)
    label_logit = jnp.einsum("btuj,jbu->btu", hidden, w_label, preferred_element_type=jnp.float32)
    return hidden, logits, log_norm, logits[..., 0] - log_norm, label_logit - log_norm


def alpha_rows(row_in, blank, lab_cum):
    def frame_step(carry, frame_in):
        blank_t, cum_t = frame_in
        alpha_t = cum_t + lax.cumlogsumexp(carry - cum_t, axis=1)
        return alpha_t + blank_t, alpha_t

    row_out, alpha = lax.scan(frame_step, row_in, (jnp.swapaxes(blank, 0, 1), jnp.swapaxes(lab_cum, 0, 1)))
    return row_out, jnp.swapaxes(alpha, 0, 1)


def beta_rows(row_in, blank, lab_cum, frame_ok, upos_ok, end_row):
    def frame_step(carry, frame_in):
        blank_t, cum_t, valid_t = frame_in
        terms = jnp.where(upos_ok, carry + blank_t + cum_t, NEG_FILL)
        beta_t = jnp.where(upos_ok, lax.cumlogsumexp(terms, axis=1, reverse=True) - cum_t, NEG_FILL)
        beta_t = jnp.where(valid_t[:, None], beta_t, end_row)
        return beta_t, beta_t

    row_out, beta = lax.scan(frame_step, row_in, (jnp.swapaxes(blank, 0, 1), jnp.swapaxes(lab_cum, 0, 1), frame_ok.T), reverse=True)
    return row_out, jnp.swapaxes(beta, 0, 1)


def occupancies(alpha, beta, beta_tail, blank, label_lp, log_prob, frame_ok, label_pos, label_len):
    beta_next = jnp.concatenate([beta[:, 1:], beta_tail[:, None]], axis=1)
    beta_right = jnp.concatenate([beta[:, :, 1:], jnp.full(beta.shape[:2] + (1,), NEG_FILL, jnp.float32)], axis=2)
    shift = log_prob[:, None, None]
    cell_ok = frame_ok[:, :, None] & (label_pos[None, None, :] <= label_len[:, None, None])
    label_ok = cell_ok & (label_pos[None, None, :] < label_len[:, None, None])
    occ_blank = jnp.where(cell_ok, jnp.exp(alpha + blank + beta_next - shift), 0.0)
    occ_label = jnp.where(label_ok, jnp.exp(alpha + label_lp + beta_right - shift), 0.0)
    return occ_blank, occ_label


def joint_backward(enc_loc, hidden, logits, log_norm, lab_ids, occ_blank, occ_label, w_enc, w_out):
    vocab = jnp.arange(w_out.shape[1])
    softmax_p = jnp.exp(logits - log_norm[..., None])
    grad_logits = (softmax_p * (occ_blank + occ_label)[..., None] - jnp.where(vocab == 0, occ_blank[..., None], 0.0) - jnp.where(vocab == lab_ids[:, None, :, None], occ_label[..., None], 0.0)).astype(jnp.bfloat16)
    grad_hidden = jnp.einsum("btuv,jv->btuj", grad_logits, w_out, preferred_element_type=jnp.float32)
    grad_w_out = jnp.einsum("btuj,btuv->jv", hidden, grad_logits, preferred_element_type=jnp.float32)
    grad_pre = grad_hidden * (1.0 - jnp.square(hidden.astype(jnp.float32)))
    grad_act_enc = jnp.sum(grad_pre, axis=2).astype(jnp.bfloat16)
    grad_enc = jnp.einsum("btj,hj->bth", grad_act_enc, w_enc, preferred_element_type=jnp.float32).astype(jnp.bfloat16)
    grad_w_enc = jnp.einsum("bth,btj->hj", enc_loc, grad_act_enc, preferred_element_type=jnp.float32)
    return grad_enc, grad_w_enc, grad_w_out, jnp.sum(grad_pre, axis=1)


def solution(mesh):
    n_seq = mesh.shape["seq"]
    to_right = [(src, src + 1) for src in range(n_seq - 1)]
    to_left = [(src + 1, src) for src in range(n_seq - 1)]
    utt_rows = P(("part", "data"))
    utt_mats = P(("part", "data"), None)
    utt_cube = P(("part", "data"), None, None)
    enc_spec = P(("part", "data"), "seq", None)
    weight_in = P(None, None)
    weight_out = P("part", None)

    def body(enc_loc, pred_loc, w_enc, w_pred, w_out, labels, frame_len, label_len):
        n_utt, t_loc, _ = enc_loc.shape
        n_upos = pred_loc.shape[1]
        seq_pos = lax.axis_index("seq")
        lab_ids = jnp.concatenate([labels, jnp.zeros((n_utt, 1), jnp.int32)], axis=1)
        hidden, logits, log_norm, blank, label_lp = joint_forward(enc_loc, pred_loc, w_enc, w_pred, w_out, lab_ids)
        lab_cum = jnp.concatenate([jnp.zeros((n_utt, t_loc, 1), jnp.float32), jnp.cumsum(label_lp[:, :, :-1], axis=2)], axis=2)
        label_pos = jnp.arange(n_upos)
        frame_pos = seq_pos * t_loc + jnp.arange(t_loc)
        frame_ok = frame_pos[None, :] < frame_len[:, None]
        upos_ok = label_pos[None, :] <= label_len[:, None]
        start_row = jnp.broadcast_to(jnp.where(label_pos == 0, 0.0, NEG_FILL), (n_utt, n_upos)).astype(jnp.float32)
        end_row = jnp.where(label_pos[None, :] == label_len[:, None], 0.0, NEG_FILL).astype(jnp.float32)

        def alpha_hop(hop_idx, row_in):
            row_out, _ = alpha_rows(row_in, blank, lab_cum)
            received = lax.ppermute(row_out, "seq", to_right)
            return jnp.where(seq_pos == 0, start_row, received)

        alpha_in = lax.fori_loop(0, n_seq - 1, alpha_hop, start_row)
        _, alpha = alpha_rows(alpha_in, blank, lab_cum)
        last_cell = (frame_pos[None, :, None] == frame_len[:, None, None] - 1) & (label_pos[None, None, :] == label_len[:, None, None])
        log_prob = lax.psum(jnp.sum(jnp.where(last_cell, alpha + blank, 0.0), axis=(1, 2)), "seq")

        def beta_hop(hop_idx, row_in):
            row_out, _ = beta_rows(row_in, blank, lab_cum, frame_ok, upos_ok, end_row)
            received = lax.ppermute(row_out, "seq", to_left)
            return jnp.where(seq_pos == n_seq - 1, end_row, received)

        beta_in = lax.fori_loop(0, n_seq - 1, beta_hop, end_row)
        _, beta = beta_rows(beta_in, blank, lab_cum, frame_ok, upos_ok, end_row)
        occ_blank, occ_label = occupancies(alpha, beta, beta_in, blank, label_lp, log_prob, frame_ok, label_pos, label_len)
        grad_enc, grad_w_enc, grad_w_out, act_pred_part = joint_backward(enc_loc, hidden, logits, log_norm, lab_ids, occ_blank, occ_label, w_enc, w_out)
        act_pred_grad = lax.psum(act_pred_part, "seq").astype(jnp.bfloat16)
        grad_pred = jnp.einsum("buj,hj->buh", act_pred_grad, w_pred, preferred_element_type=jnp.float32)
        grad_w_pred = jnp.einsum("buh,buj->hj", pred_loc, act_pred_grad, preferred_element_type=jnp.float32)
        grad_w_enc = lax.psum(grad_w_enc, ("data", "seq"))
        grad_w_out = lax.psum(grad_w_out, ("data", "seq"))
        grad_w_pred = lax.psum(grad_w_pred, "data")
        return -log_prob, grad_enc, grad_pred, grad_w_enc, grad_w_pred, grad_w_out

    return jax.shard_map(body, mesh=mesh, in_specs=(enc_spec, utt_cube, weight_in, weight_in, weight_in, utt_mats, utt_rows, utt_rows), out_specs=(utt_rows, enc_spec, utt_cube, weight_out, weight_out, weight_out), check_vma=False)
```

profile of v0, /device:TPU:0, one launch (start us, length us, event | category | flops | bytes accessed | tf_op | source)
XLA Modules:
  0.0 574.2 jit_solution(2825327534350157290)
XLA Ops:
  8.8 1.7 copy.27
  10.5 2.9 fusion.45
  13.3 3.3 fusion.51
  16.6 8.9 %tanh_convert_fusion = bf16[16,24,24,640]{3,2,1,0:T(8,128)(2,1)} fusion(f32[16,24,640]{2,1,0:T(8,128)} %fusion.51, f32[16,24,640]{2,1,0:T(8,128)} %fusion.45), kind=kLoop, calls=%fused_computation.44 | loop fusion | flops 11796480 | bytes 13762560 | tf_op jit(solution)/shard_map/convert_element_type | solution.py:12
  25.5 21.1 %fusion.68 = (f32[16,24,24]{2,1,0:T(8,128)S(1)}, f32[16,24,24,1024]{3,2,1,0:T(8,128)}) fusion(bf16[640,1024]{1,0:T(8,128)(2,1)} %param.24, f32[16,24,640]{2,1,0:T(8,128)} %fusion.51, f32[16,24,640]{2,1,0:T(8,128)} %fusion.45), kind=kOutput, calls=%fused_computation.113 | convolution fusion | flops 12100819968 | bytes 41062400 | tf_op jit(solution)/shard_map/btuj,jv->btuv/dot_general | solution.py:13
  46.6 2.4 gather_fusion
  49.2 8.3 %fusion.25 = f32[16,24,1,24]{3,2,1,0:T(1,128)S(1)} fusion(bf16[16,24,24,640]{3,2,1,0:T(8,128)(2,1)} %tanh_convert_fusion, bf16[640,16,24,1]{0,2,1,3:T(8,128)(2,1)S(1)} %select_bitcast_fusion.1), kind=kOutput, calls=%fused_computation.49 | convolution fusion | flops 11796480 | bytes 12324864 | tf_op jit(solution)/shard_map/btuj,jbu->btu/dot_general | solution.py:16
  57.7 17.8 %exponential_reduce_fusion = f32[16,24,24]{2,1,0:T(8,128)S(1)} fusion(f32[16,24,24,1024]{3,2,1,0:T(8,128)} %get-tuple-element.875, f32[16,24,24]{2,1,0:T(8,128)S(1)} %is-finite_select_fusion), kind=kLoop, calls=%fused_computation.42 | loop fusion | flops 18865152 | bytes 37822464 | tf_op jit(solution)/shard_map/reduce_sum | solution.py:14
  76.2 2.9 reduce_window_sum.11
  79.2 3.6 slice_reduce_fusion
  83.1 1.0 sub.105
  84.9 91.1 %while.108 = (s32[]{:T(128)}, f32[16,24]{1,0:T(8,128)S(1)}, pred[]{:T(512)}, f32[16,24,24]{2,0,1:T(8,128)S(1)}, f32[16,24,24]{2,0,1:T(8,128)S(1)}, /*index=5*/s3...) while((s32[]{:T(128)}, f32[16,24]{1,0:T(8,128)S(1)}, ...), condition=%wide.region_17.18_spmd.clone.clone, body=%wide.region_13.17_spmd.clone.clone.sunk | while | flops 75653 | bytes 28431 | solution.py:106
  85.1 25.3 %while.111 = (s32[]{:T(128)}, f32[16,24]{1,0:T(8,128)S(1)}, pred[24,16]{1,0:T(8,128)(4,1)S(1)}, f32[24,16,24]{2,1,0:T(8,128)S(1)}, f32[24,16,24]{2,1,0:T(8,128)S...) while((s32[]{:T(128)}, f32[16,24]{1,0:T(8,128)S(1)}, ...), condition=%wide.region_16.16_spmd, body=%wide.region_14.15_spmd.sunk | while | flops 72963 | bytes 16305 | solution.py:38
  110.5 1.3 collective-permute-start
  111.8 2.2 collective-permute-done
  114.2 25.3 %while.111 = (s32[]{:T(128)}, f32[16,24]{1,0:T(8,128)S(1)}, pred[24,16]{1,0:T(8,128)(4,1)S(1)}, f32[24,16,24]{2,1,0:T(8,128)S(1)}, f32[24,16,24]{2,1,0:T(8,128)S...) while((s32[]{:T(128)}, f32[16,24]{1,0:T(8,128)S(1)}, ...), condition=%wide.region_16.16_spmd, body=%wide.region_14.15_spmd.sunk | while | flops 72963 | bytes 16305 | solution.py:38
  139.6 1.3 collective-permute-start
  140.9 4.5 collective-permute-done
  145.6 25.3 %while.111 = (s32[]{:T(128)}, f32[16,24]{1,0:T(8,128)S(1)}, pred[24,16]{1,0:T(8,128)(4,1)S(1)}, f32[24,16,24]{2,1,0:T(8,128)S(1)}, f32[24,16,24]{2,1,0:T(8,128)S...) while((s32[]{:T(128)}, f32[16,24]{1,0:T(8,128)S(1)}, ...), condition=%wide.region_16.16_spmd, body=%wide.region_14.15_spmd.sunk | while | flops 72963 | bytes 16305 | solution.py:38
  170.9 1.3 collective-permute-start
  172.2 3.7 collective-permute-done
  176.0 47.0 %while.109 = (s32[]{:T(128)}, f32[16,24]{1,0:T(8,128)S(1)}, f32[24,16,24]{2,0,1:T(8,128)S(1)}, pred[24,16]{1,0:T(8,128)(4,1)S(1)}, f32[24,16,24]{2,1,0:T(8,128)}...) while((s32[]{:T(128)}, f32[16,24]{1,0:T(8,128)S(1)}, ...), condition=%wide.region_20.21_spmd.clone.clone, body=%wide.region_18.20_spmd.clone.clone.sunk | while | flops 76803 | bytes 21905 | solution.py:38
  176.8 0.9 reduce_window.50
  178.8 0.9 reduce_window.50
  180.7 0.9 reduce_window.50
  224.5 1.0 iota_compare_fusion.4
  225.6 58.8 %while.106 = (s32[]{:T(128)}, f32[16,24]{1,0:T(8,128)S(1)}, pred[]{:T(512)}, f32[16,24,24]{2,0,1:T(8,128)S(1)}, f32[16,24,24]{2,0,1:T(8,128)S(1)}, /*index=5*/f3...) while((s32[]{:T(128)}, f32[16,24]{1,0:T(8,128)S(1)}, pred[]{:T(512)}, ...), condition=%wide.region_7.8_spmd.clone, body=%wide.region_3.7_spmd.clone.sunk | while | flops 72196 | bytes 23423 | solution.py:96
  225.6 15.3 %while.110 = (s32[]{:T(128)}, f32[16,24]{1,0:T(8,128)S(1)}, f32[24,16,24]{2,1,0:T(8,128)S(1)}, f32[24,16,24]{2,1,0:T(8,128)S(1)}, s32[]{:T(128)}, /*index=5*/f32[]{:T(128)}) while((s32[]{:T(128)}, f32[16,24]{1,0:T(8,128)S(1)}, f32[24,16,24]{2,1,0:T(8,128)S(1)}, f32[24,16,24]{2,1,0:T(8,128)S(1)}, s32[]{:T(128)}, /*index=5*/f32[]{:T(128)}) %tuple.224), condition=%wide.region_6.6_spmd, body=%wide.region_4.5_spmd.sunk | while | flops 71810 | bytes 13913 | solution.py:26
  240.9 4.3 collective-permute-start.1
  246.0 15.3 %while.110 = (s32[]{:T(128)}, f32[16,24]{1,0:T(8,128)S(1)}, f32[24,16,24]{2,1,0:T(8,128)S(1)}, f32[24,16,24]{2,1,0:T(8,128)S(1)}, s32[]{:T(128)}, /*index=5*/f32[]{:T(128)}) while((s32[]{:T(128)}, f32[16,24]{1,0:T(8,128)S(1)}, f32[24,16,24]{2,1,0:T(8,128)S(1)}, f32[24,16,24]{2,1,0:T(8,128)S(1)}, s32[]{:T(128)}, /*index=5*/f32[]{:T(128)}) %tuple.224), condition=%wide.region_6.6_spmd, body=%wide.region_4.5_spmd.sunk | while | flops 71810 | bytes 13913 | solution.py:26
  261.4 2.3 collective-permute-start.1
  264.5 15.3 %while.110 = (s32[]{:T(128)}, f32[16,24]{1,0:T(8,128)S(1)}, f32[24,16,24]{2,1,0:T(8,128)S(1)}, f32[24,16,24]{2,1,0:T(8,128)S(1)}, s32[]{:T(128)}, /*index=5*/f32[]{:T(128)}) while((s32[]{:T(128)}, f32[16,24]{1,0:T(8,128)S(1)}, f32[24,16,24]{2,1,0:T(8,128)S(1)}, f32[24,16,24]{2,1,0:T(8,128)S(1)}, s32[]{:T(128)}, /*index=5*/f32[]{:T(128)}) %tuple.224), condition=%wide.region_6.6_spmd, body=%wide.region_4.5_spmd.sunk | while | flops 71810 | bytes 13913 | solution.py:26
  279.8 3.8 collective-permute-start.1
  284.4 33.8 %while.104 = (s32[]{:T(128)}, f32[16,24]{1,0:T(8,128)S(1)}, f32[24,16,24]{2,0,1:T(8,128)S(1)}, f32[24,16,24]{2,1,0:T(8,128)S(1)}, f32[24,16,24]{2,1,0:T(8,128)}, /*index=5*/s32[]{:T(128)}, f32[]{:T(128)}, s32[]{:T(128)}) while((s32[]{:T(128)}, f32[16,24]{1,0:T(8,128)S(1)}, f32[24,16,24]{2,0,1:T(8,128)S(1)}, f32[24,16,24]{2,1,0:T(8,128)S(1)}, ...), condition=%wide.region_10.11_spmd, body=%wide.region_8.10_spmd.sunk | while | flops 72194 | bytes 21617 | solution.py:26
  318.6 8.0 %psum.35 = f32[16]{0:T(128)S(1)} all-reduce(f32[16]{0:T(128)S(1)} %select_reduce_fusion), channel_id=1, replica_groups=mesh['part'=1,'data'=2,'seq'=4] {'seq'}, use_global_device_ids=true, to_apply=%region_12.13 | all-reduce | flops 16 | bytes 128 | tf_op jit(solution)/shard_map/psum | solution.py:99
  326.6 1.2 fusion.65
  327.9 33.7 %fusion.21 = (f32[16,24,640]{2,1,0:T(8,128)}, bf16[16,24,640]{2,1,0:T(8,128)(2,1)S(1)}) fusion(f32[16,24,640]{2,1,0:T(8,128)} %fusion.51, f32[16,24,640]{2,1,0:T(8,128)S(1)} %copy-done.2, bf16[640,1024]{1,0:T(8,128)(2,1)} %param.24, f32[16,24,24,1024]{3,2,1,0:T(8,128)} %get-tuple-element.875, f32[16,24,24]{2,1,0:T(8,128)S(1)} %get-tuple-element.864, ...), kind=kOutput, calls=%fused_computation.45 | convolution fusion | flops 12192350208 | bytes 43041792 | tf_op jit(solution)/shard_map/btuv,jv->btuj/dot_general | solution.py:57
  361.6 27.1 %fusion.31 = f32[640,1024]{1,0:T(8,128)} fusion(f32[16,24,640]{2,1,0:T(8,128)S(1)} %copy-done.3, f32[16,24,640]{2,1,0:T(8,128)S(1)} %copy-done.2, f32[16,24,24,1024]{3,2,1,0:T(8,128)} %get-tuple-element.875, f32[16,24,24]{2,1,0:T(8,128)S(1)} %get-tuple-element.864, f32[16,24,24]{2,1,0:T(8,128)S(1)} %get-tuple-element.863, ...), kind=kOutput, calls=%fused_computation.58 | convolution fusion | flops 12157452288 | bytes 42877952 | tf_op jit(solution)/shard_map/btuj,btuv->jv/dot_general | solution.py:58
  388.7 2.4 convolution_bitcast_fusion.1
  391.2 41.3 %all-reduce.11 = bf16[16,24,640]{2,1,0:T(8,128)(2,1)S(1)} all-reduce(f32[16,24,640]{2,1,0:T(8,128)} %get-tuple-element.784), channel_id=1, replica_groups=mesh['part'=1,'data'=2,'seq'=4] {'seq'}, use_global_device_ids=true, to_apply=%region_23.24 | all-reduce | flops 245760 | bytes 1474560 | tf_op jit(solution)/shard_map/psum | solution.py:110
  432.5 3.6 convolution_bitcast_fusion
  436.6 2.7 convolution_convert_fusion
  439.3 2.0 fusion.35
  441.3 48.4 %all-reduce.10.cloned.1.call-done = (f32[1024,640]{0,1:T(8,128)}, f32[640,1024]{1,0:T(8,128)}) async-done(((f32[1024,640]{0,1:T(8,128)}, f32[640,1024]{1,0:T(8,128)}), (f32[1024,640]{0,1:T(8,128)}, f32[640,1024]{1,0:T(8,128)})) %all-reduce.10.cloned.1.call-update) | async-done | bytes 5242896 | tf_op jit(solution)/shard_map/psum | solution.py:113
  489.7 3.2 copy.38
  492.9 67.7 %all-reduce.8.cloned.1.call-done = f32[1024,640]{0,1:T(8,128)} async-done(((f32[1024,640]{0,1:T(8,128)}), f32[1024,640]{0,1:T(8,128)}) %all-reduce.8.cloned.1.call-update) | async-done | bytes 2621456 | tf_op jit(solution)/shard_map/psum | solution.py:115
  560.6 3.2 copy.39
  563.8 3.6 copy.115
  (836 shorter events, 207.0 us)
Async XLA Ops:
  7.2 3.3 copy-start
  7.2 482.5 %all-reduce.10.cloned.1.call-start = ((), (), s32[]{:S(2)}) async-start(), calls=%async_computation.1 | async-start | bytes 10485760 | tf_op jit(solution)/shard_map/psum | solution.py:113
  57.6 25.2 %copy-start.7 = (s32[16]{0:T(128)S(1)}, s32[16]{0:T(128)}, u32[]{:S(2)}) copy-start(s32[16]{0:T(128)} %param.26) | copy-start | bytes 196
  57.6 25.3 %copy-start.5 = (s32[16]{0:T(128)S(1)}, s32[16]{0:T(128)}, u32[]{:S(2)}) copy-start(s32[16]{0:T(128)} %param.27) | copy-start | bytes 196
  75.4 252.4 %copy-start.2 = (f32[16,24,640]{2,1,0:T(8,128)S(1)}, f32[16,24,640]{2,1,0:T(8,128)}, u32[]{:S(2)}) copy-start(f32[16,24,640]{2,1,0:T(8,128)} %fusion.45) | copy-start | bytes 2949124
  110.5 3.5 collective-permute-start
  139.6 5.7 %collective-permute-start = (f32[16,24]{1,0:T(8,128)S(1)}, f32[16,24]{1,0:T(8,128)S(1)}, u32[]{:S(2)}, u32[]{:S(2)}) collective-permute-start(f32[16,24]{1,0:T(8,128)S(1)} %get-tuple-element.1114), channel_id=1, source_target_pairs={{1,0},{2,1},{3,2},{5,4},{6,5},{7,6}} | collective-permute-start | bytes 4616 | tf_op jit(solution)/shard_map/while/body/eval_jaxpr/ppermute | solution.py:103
  170.9 5.0 collective-permute-start
  240.9 5.1 collective-permute-start.1
  261.4 3.1 collective-permute-start.1
  279.8 4.6 collective-permute-start.1
  327.8 33.7 %copy-start.3 = (f32[16,24,640]{2,1,0:T(8,128)S(1)}, f32[16,24,640]{2,1,0:T(8,128)}, u32[]{:S(2)}) copy-start(f32[16,24,640]{2,1,0:T(8,128)} %fusion.51) | copy-start | bytes 2949124
  327.9 33.7 %copy-start.4 = (f32[16,24,24]{2,1,0:T(8,128)S(1)}, f32[16,24,24]{2,1,0:T(8,128)}, u32[]{:S(2)}) copy-start(f32[16,24,24]{2,1,0:T(8,128)} %get-tuple-element.866) | copy-start | bytes 110596
  327.9 33.7 %copy-start.6 = (pred[16,24,1024]{2,1,0:T(8,128)(4,1)S(1)}, pred[16,24,1024]{2,1,0:T(8,128)(4,1)}, u32[]{:S(2)}) copy-start(pred[16,24,1024]{2,1,0:T(8,128)(4,1)} %iota_compare_fusion.4) | copy-start | bytes 1179652
  361.6 27.1 %copy-start.9 = (bf16[16,24,640]{2,1,0:T(8,128)(2,1)}, bf16[16,24,640]{2,1,0:T(8,128)(2,1)S(1)}, u32[]{:S(2)}) copy-start(bf16[16,24,640]{2,1,0:T(8,128)(2,1)S(1)} %get-tuple-element.785) | copy-start | bytes 1474564
  361.6 27.1 %copy-start.8 = (bf16[16,24,1024]{2,1,0:T(8,128)(2,1)S(1)}, bf16[16,24,1024]{2,1,0:T(8,128)(2,1)}, u32[]{:S(2)}) copy-start(bf16[16,24,1024]{2,1,0:T(8,128)(2,1)} %param.20) | copy-start | bytes 2359300
  391.1 48.2 %copy-start.1 = (bf16[1024,640]{1,0:T(8,128)(2,1)S(1)}, bf16[1024,640]{1,0:T(8,128)(2,1)}, u32[]{:S(2)}) copy-start(bf16[1024,640]{1,0:T(8,128)(2,1)} %param.23) | copy-start | bytes 3932164
  391.1 169.5 %all-reduce.8.cloned.1.call-start = ((), (), s32[]{:S(2)}) async-start(), calls=%async_computation | async-start | bytes 5242880 | tf_op jit(solution)/shard_map/psum | solution.py:115
Sparse Core Ops, SparseCore 0:
  391.2 98.4 all-reduce.9
  492.0 68.6 all-reduce.7
where the time goes:
time: 578 us; the launch traced here: 574 us
  other arithmetic  234 us (40%)
  waiting for transfers between devices  129 us (22%)
  matrix products  107 us (19%)
  blocking collectives  49.3 us (9%)
  local copies, waits for them, and re-layouts  23.7 us (4%)
  starting transfers between devices  14.3 us (2%)
  between operations  14.3 us (2%)
    another operation x96, other arithmetic, frame_step(): lax.cumlogsumexp(terms, axis=1, reverse=True) - cum_t  90.2 us
    psum x1, waiting for transfers between devices, body(): grad_w_pred = lax.psum(grad_w_pred, 'data')  67.7 us
    another operation x96, other arithmetic, frame_step(): alpha_t = cum_t + lax.cumlogsumexp(carry - cum_t, axis=1)  59.2 us
    psum x1, waiting for transfers between devices, body(): grad_w_enc = lax.psum(grad_w_enc, ('data', 'seq'))  48.4 us
    psum x1, blocking collectives, body(): act_pred_grad = lax.psum(act_pred_part, 'seq').astype(jnp.bfloat16)  41.3 us
    dot_general x1, matrix products, joint_backward(): jnp.einsum('btuv,jv->btuj', grad_logits, w_out, preferred_element_type=jn...  33.7 us
    dot_general x1, matrix products, joint_backward(): jnp.einsum('btuj,btuv->jv', hidden, grad_logits, preferred_element_type=j...  27.1 us
    dot_general x1, matrix products, joint_forward(): jnp.einsum('btuj,jv->btuv', hidden, w_out, preferred_element_type=jnp.flo...  21.1 us
  transfers between devices with their start and end apart: 8, of which 8 were waited for; matrix products, arithmetic and copies ran while one was open for 2% of the time, Pallas kernels for 0%

commit v1 on v0

v1 whole, which is shorter than its diff:
```python
import functools

import jax
import jax.numpy as jnp
from jax import lax
from jax.experimental import pallas as pl
from jax.experimental.pallas import tpu as pltpu
from jax.sharding import PartitionSpec as P

NEG = -1e30
LOG2E = 1.4426950408889634
LN2 = 0.6931471805599453
F32 = jnp.float32
BF16 = jnp.bfloat16
MESH = pl.DeviceIdType.MESH
VMEM_FULL = 67_000_000
N_UTT = 16
T_LOC = 24
N_UP = 24
UG = 3
N_SEQ = 4
T_ALL = T_LOC * N_SEQ
N_DIAG = T_ALL + N_UP - 1
ROWS = 8 * T_LOC


def dot(lhs, rhs, dims=((1,), (0,))):
    return lax.dot_general(lhs, rhs, (dims, ((), ())), preferred_element_type=F32)


def forward_kernel(enc, pred, w_enc, w_pred, w_out, lab, e_out, h_out, stat_out, sum_out, act_e, act_p):
    utt = pl.program_id(0)

    @pl.when(utt == 0)
    def _():
        act_e[...] = dot(enc[...], w_enc[...]).astype(BF16).astype(F32)
        act_p[...] = dot(pred[...], w_pred[...]).astype(BF16).astype(F32)
        stat_out[...] = jnp.zeros_like(stat_out)
        sum_out[...] = jnp.ones_like(sum_out)

    row = pl.multiple_of(utt * N_UP, 8)
    a_utt = act_e[pl.ds(row, T_LOC), :]
    lane = lax.broadcasted_iota(jnp.int32, (8, 128), 1)
    for ug in range(UG):
        c_grp = act_p[pl.ds(row + 8 * ug, 8), :]
        lab_grp = lab[pl.ds(row + 8 * ug, 8), :]
        pre = jnp.concatenate([a_utt[t:t + 1, :] + c_grp for t in range(T_LOC)], axis=0)
        hid = jnp.tanh(pre).astype(BF16)
        h_out[0, ug] = hid
        z = dot(hid, w_out[...])
        top = jnp.max(z, axis=1, keepdims=True)
        e = jnp.exp2((z - top) * LOG2E)
        e_out[0, ug] = e
        tot = jnp.sum(e, axis=1, keepdims=True)
        mask = jnp.concatenate([lab_grp - 128 * k == lane for k in range(z.shape[1] // 128)], axis=1)
        z3 = z.reshape(T_LOC, 8, z.shape[1])
        picked = jnp.sum(jnp.where(mask[None], z3, 0.0), axis=2, keepdims=True).reshape(ROWS, 1)
        log_tot = jnp.log2(tot)
        blank = (z[:, 0:1] - top) * LOG2E - log_tot
        label = (picked - top) * LOG2E - log_tot
        for t4 in range(T_LOC // 4):
            cur = stat_out[ug * 6 + t4]
            for k in range(4):
                rows = slice((t4 * 4 + k) * 8, (t4 * 4 + k) * 8 + 8)
                cur = jnp.where(lane == utt + 32 * k, blank[rows], cur)
                cur = jnp.where(lane == utt + 32 * k + 16, label[rows], cur)
            stat_out[ug * 6 + t4] = cur
        for t in range(T_LOC):
            sum_out[ug * T_LOC + t] = jnp.where(lane == utt, tot[t * 8:t * 8 + 8], sum_out[ug * T_LOC + t])


def joint_forward(enc, pred, w_enc, w_pred, w_out, lab):
    n_v = w_out.shape[1]
    n_j = w_out.shape[0]
    full = lambda shape: pl.BlockSpec(shape, lambda i: (0,) * len(shape), pipeline_mode=pl.Buffered(1))
    return pl.pallas_call(
        forward_kernel,
        grid=(N_UTT,),
        in_specs=[full(enc.shape), full(pred.shape), full(w_enc.shape), full(w_pred.shape), full(w_out.shape), full(lab.shape)],
        out_specs=[
            pl.BlockSpec((1, UG, ROWS, n_v), lambda i: (i, 0, 0, 0)),
            pl.BlockSpec((1, UG, ROWS, n_j), lambda i: (i, 0, 0, 0)),
            pl.BlockSpec((UG * 6, 8, 128), lambda i: (0, 0, 0)),
            pl.BlockSpec((UG * T_LOC, 8, 128), lambda i: (0, 0, 0)),
        ],
        out_shape=[
            jax.ShapeDtypeStruct((N_UTT, UG, ROWS, n_v), F32),
            jax.ShapeDtypeStruct((N_UTT, UG, ROWS, n_j), BF16),
            jax.ShapeDtypeStruct((UG * 6, 8, 128), F32),
            jax.ShapeDtypeStruct((UG * T_LOC, 8, 128), F32),
        ],
        scratch_shapes=[pltpu.VMEM((N_UTT * T_LOC, n_j), F32), pltpu.VMEM((N_UTT * N_UP, n_j), F32)],
        compiler_params=pltpu.CompilerParams(vmem_limit_bytes=VMEM_FULL),
        name="joint_forward",
    )(enc, pred, w_enc, w_pred, w_out, lab)


def lae2(x, y):
    return jnp.maximum(x, y) + jnp.log2(1.0 + jnp.exp2(-jnp.abs(x - y)))


def lattice_kernel(stat, sums, flen, llen, q0_out, q1_out, r_out, loss_out, gath, s_blank, s_label, s_alpha, s_beta, send_sem, recv_sem):
    me = lax.axis_index("seq")
    barrier = pltpu.get_barrier_semaphore()
    for off in range(1, N_SEQ):
        pl.semaphore_signal(barrier, inc=1, device_id={"seq": lax.rem(me + off, N_SEQ)}, device_id_type=MESH)
    pl.semaphore_wait(barrier, N_SEQ - 1)
    copies = []
    for off in range(1, N_SEQ):
        cp = pltpu.make_async_remote_copy(
            src_ref=stat, dst_ref=gath.at[off - 1], send_sem=send_sem.at[off - 1], recv_sem=recv_sem.at[off - 1],
            device_id={"seq": lax.rem(me + off, N_SEQ)}, device_id_type=MESH)
        cp.start()
        copies.append(cp)

    sub = lax.broadcasted_iota(jnp.int32, (8, 128), 0)
    sub24 = lax.broadcasted_iota(jnp.int32, (N_UP, 128), 0)
    tb = flen[...]
    ub = llen[...]
    n_pad = s_blank.shape[0]

    def fill(i, c):
        s_blank[pl.ds(pl.multiple_of(i * 8, 8), 8), :] = jnp.full((8, 128), NEG, F32)
        s_label[pl.ds(pl.multiple_of(i * 8, 8), 8), :] = jnp.full((8, 128), NEG, F32)
        return c

    lax.fori_loop(0, n_pad // 8, fill, 0, unroll=8)
    end_grp = [jnp.where(sub + 8 * ug == ub, 0.0, NEG) for ug in range(UG)]
    for t in range(T_ALL, T_ALL + N_UP):
        for ug in range(UG):
            s_blank[pl.ds(t * N_UP + 200 * ug, 8, stride=25), :] = end_grp[ug]

    def place(src, src_seq):
        for t4 in range(T_LOC // 4):
            for ug in range(UG):
                val = src[ug * 6 + t4]
                in_u = sub + 8 * ug <= ub
                in_l = sub + 8 * ug < ub
                for k in range(4):
                    t = src_seq * T_LOC + t4 * 4 + k
                    bl = val if k == 0 else pltpu.roll(val, 128 - 32 * k, 1)
                    la = pltpu.roll(val, 112 - 32 * k, 1)
                    ok = t < tb
                    s_blank[pl.ds(t * N_UP + 200 * ug, 8, stride=25), :] = jnp.where(ok, jnp.where(in_u, bl, NEG), end_grp[ug])
                    s_label[pl.ds(t * N_UP + 200 * ug, 8, stride=25), :] = jnp.where(ok & in_l, la, NEG)

    place(stat, me)
    for off in range(1, N_SEQ):
        copies[off - 1].wait_recv()
        place(gath.at[off - 1], lax.rem(me + N_SEQ - off, N_SEQ))

    alpha0 = jnp.where(sub24 == 0, 0.0, NEG)
    s_alpha[pl.ds(0, N_UP), :] = alpha0
    beta_end = jnp.where(sub24 == jnp.concatenate([ub] * UG, axis=0), 0.0, NEG)
    s_beta[pl.ds(N_DIAG * N_UP, N_UP), :] = beta_end
    s_beta[pl.ds((N_DIAG + 1) * N_UP, 8), :] = jnp.full((8, 128), NEG, F32)

    def wave(i, carry):
        alpha, beta = carry
        row = pl.multiple_of(i * N_UP, 8)
        x = alpha + s_blank[pl.ds(row, N_UP), :]
        y = alpha + s_label[pl.ds(row, N_UP), :]
        y = jnp.where(sub24 == 0, NEG, pltpu.roll(y, 1, 0))
        alpha = lae2(x, y)
        s_alpha[pl.ds(pl.multiple_of(row + N_UP, 8), N_UP), :] = alpha
        brow = pl.multiple_of((N_DIAG - 1 - i) * N_UP, 8)
        bx = beta + s_blank[pl.ds(brow, N_UP), :]
        by = pltpu.roll(beta, N_UP - 1, 0) + s_label[pl.ds(brow, N_UP), :]
        beta = lae2(bx, by)
        s_beta[pl.ds(brow, N_UP), :] = beta
        return alpha, beta

    _, beta = lax.fori_loop(0, N_DIAG, wave, (alpha0, beta_end), unroll=7)
    log_p = beta[0:1, :]
    loss_out[...] = jnp.broadcast_to(-LN2 * log_p, (8, 128))
    for t in range(T_LOC):
        tg = me * T_LOC + t
        for ug in range(UG):
            base = tg * N_UP + 200 * ug
            grp = lambda ref, off: ref[pl.ds(base + off, 8, stride=25), :]
            al = grp(s_alpha, 0) - log_p
            ok = (tg < tb) & (sub + 8 * ug <= ub)
            q0 = jnp.where(ok, jnp.exp2(al + grp(s_blank, 0) + grp(s_beta, 24)), 0.0)
            q1 = jnp.where(ok, jnp.exp2(al + grp(s_label, 0) + grp(s_beta, 25)), 0.0)
            idx = ug * T_LOC + t
            q0_out[idx] = q0
            q1_out[idx] = q1
            r_out[idx] = (q0 + q1) / sums[idx]
    for cp in copies:
        cp.wait_send()


def lattice(stat, sums, flen, llen):
    vm = pl.BlockSpec(memory_space=pltpu.VMEM)
    n_rows = (T_ALL + 2 * N_UP) * N_UP
    return pl.pallas_call(
        lattice_kernel,
        in_specs=[vm] * 4,
        out_specs=[vm] * 4,
        out_shape=[jax.ShapeDtypeStruct(sums.shape, F32)] * 3 + [jax.ShapeDtypeStruct((8, 128), F32)],
        scratch_shapes=[pltpu.VMEM((N_SEQ - 1,) + stat.shape, F32)] + [pltpu.VMEM((n_rows, 128), F32)] * 4
        + [pltpu.SemaphoreType.DMA((N_SEQ - 1,)), pltpu.SemaphoreType.DMA((N_SEQ - 1,))],
        compiler_params=pltpu.CompilerParams(collective_id=0, has_side_effects=True),
        name="lattice",
    )(stat, sums, flen, llen)


U_STEP = 4


def backward_kernel(e_ref, h_ref, q0_ref, q1_ref, r_ref, lab, w_out_t, da_out, dc_out, dw_out, dz_scr):
    step = pl.program_id(0)
    lane = lax.broadcasted_iota(jnp.int32, (8, 128), 1)
    n_v = w_out_t.shape[0]
    n_j = w_out_t.shape[1]
    for i in range(U_STEP):
        utt = step * U_STEP + i
        row = pl.multiple_of(utt * N_UP, 8)
        acc = None
        for ug in range(UG):
            shift = 128 - utt
            col = lambda ref: pltpu.roll(ref[ug * T_LOC:(ug + 1) * T_LOC].reshape(ROWS, 128), shift, 1)[:, 0:1].reshape(T_LOC, 8, 1)
            q0, q1, r = col(q0_ref), col(q1_ref), col(r_ref)
            lab_grp = lab[pl.ds(row + 8 * ug, 8), :]
            mask = jnp.concatenate([lab_grp - 128 * k == lane for k in range(n_v // 128)], axis=1)
            first = jnp.concatenate([lane + 128 * k == 0 for k in range(n_v // 128)], axis=1)
            e3 = e_ref[i, ug].reshape(T_LOC, 8, n_v)
            dz = e3 * r - jnp.where(mask[None], q1, 0.0) - jnp.where(first[None], q0, 0.0)
            dz = dz.reshape(ROWS, n_v).astype(BF16)
            base = (i * UG + ug) * ROWS
            dz_scr[base:base + ROWS, :] = dz
            dh = dot(dz, w_out_t[...])
            hid = h_ref[i, ug].astype(F32)
            ds = (dh * (1.0 - hid * hid)).reshape(T_LOC, 8, n_j)
            dc_out[i, ug * 8:ug * 8 + 8, :] = jnp.sum(ds, axis=0)
            acc = ds if acc is None else acc + ds
        da_out[i] = jnp.sum(acc, axis=1).astype(BF16)
    part = dot(h_ref[...].reshape(U_STEP * UG * ROWS, n_j), dz_scr[...], ((0,), (0,)))

    @pl.when(step == 0)
    def _():
        dw_out[...] = part

    @pl.when(step > 0)
    def _():
        dw_out[...] += part


def joint_backward(e, h, q0, q1, r, lab, w_out_t):
    n_v, n_j = w_out_t.shape
    full = lambda shape: pl.BlockSpec(shape, lambda i: (0,) * len(shape), pipeline_mode=pl.Buffered(1))
    return pl.pallas_call(
        backward_kernel,
        grid=(N_UTT // U_STEP,),
        in_specs=[
            pl.BlockSpec((U_STEP, UG, ROWS, n_v), lambda i: (i, 0, 0, 0)),
            pl.BlockSpec((U_STEP, UG, ROWS, n_j), lambda i: (i, 0, 0, 0)),
            full(q0.shape), full(q1.shape), full(r.shape), full(lab.shape), full(w_out_t.shape),
        ],
        out_specs=[
            pl.BlockSpec((U_STEP, T_LOC, n_j), lambda i: (i, 0, 0)),
            pl.BlockSpec((U_STEP, N_UP, n_j), lambda i: (i, 0, 0)),
            pl.BlockSpec((n_j, n_v), lambda i: (0, 0)),
        ],
        out_shape=[
            jax.ShapeDtypeStruct((N_UTT, T_LOC, n_j), BF16),
            jax.ShapeDtypeStruct((N_UTT, N_UP, n_j), F32),
            jax.ShapeDtypeStruct((n_j, n_v), F32),
        ],
        scratch_shapes=[pltpu.VMEM((U_STEP * UG * ROWS, n_v), BF16)],
        compiler_params=pltpu.CompilerParams(vmem_limit_bytes=VMEM_FULL),
        name="joint_backward",
    )(e, h, q0, q1, r, lab, w_out_t)


def solution(mesh):
    utt_rows = P(("part", "data"))
    utt_mats = P(("part", "data"), None)
    utt_cube = P(("part", "data"), None, None)
    enc_spec = P(("part", "data"), "seq", None)
    weight_in = P(None, None)
    weight_out = P("part", None)

    def body(enc_loc, pred_loc, w_enc, w_pred, w_out, labels, frame_len, label_len):
        n_h = enc_loc.shape[2]
        lab_ids = jnp.concatenate([labels, jnp.zeros((N_UTT, 1), jnp.int32)], axis=1)
        lab = jnp.broadcast_to(lab_ids.reshape(N_UTT * N_UP, 1), (N_UTT * N_UP, 128))
        enc2 = enc_loc.reshape(N_UTT * T_LOC, n_h)
        pred2 = pred_loc.reshape(N_UTT * N_UP, n_h)
        e, h, stat, sums = joint_forward(enc2, pred2, w_enc, w_pred, w_out, lab)
        lens = lambda v: jnp.broadcast_to(jnp.tile(v, 8)[None], (8, 128))
        q0, q1, r, loss = lattice(stat, sums, lens(frame_len), lens(label_len))
        da, dc, grad_w_out = joint_backward(e, h, q0, q1, r, lab, w_out.T)
        da2 = da.reshape(N_UTT * T_LOC, -1)
        grad_enc = dot(da2, w_enc, ((1,), (1,))).astype(BF16).reshape(enc_loc.shape)
        grad_w_enc = dot(enc2, da2, ((0,), (0,)))
        dc = lax.psum(dc, "seq").astype(BF16).reshape(N_UTT * N_UP, -1)
        grad_pred = dot(dc, w_pred, ((1,), (1,))).reshape(pred_loc.shape)
        grad_w_pred = dot(pred2, dc, ((0,), (0,)))
        grad_w_enc = lax.psum(grad_w_enc, ("data", "seq"))
        grad_w_out = lax.psum(grad_w_out, ("data", "seq"))
        grad_w_pred = lax.psum(grad_w_pred, "data")
        return loss[0, :N_UTT], grad_enc, grad_pred, grad_w_enc, grad_w_pred, grad_w_out

    return jax.shard_map(body, mesh=mesh, in_specs=(enc_spec, utt_cube, weight_in, weight_in, weight_in, utt_mats, utt_rows, utt_rows), out_specs=(utt_rows, enc_spec, utt_cube, weight_out, weight_out, weight_out), check_vma=False)
```

time: 578 us -> 281 us (0.49)
  other arithmetic: 234 us -> 0 us
  matrix products: 107 us -> 10.7 us
  Pallas kernels: 0 us -> 81.8 us
  starting transfers between devices: 14.3 us -> 0.08 us
  waiting for transfers between devices: 129 us -> 116 us
  blocking collectives: 49.3 us -> 40.7 us
  local copies, waits for them, and re-layouts: 23.7 us -> 17.1 us
    another operation x193 -> x0, other arithmetic: 152 us -> none  [the longest x96 90.2 us: frame_step(): lax.cumlogsumexp(terms, axis=1, reverse=True) - cum_t]
    dot_general x10 -> x4, matrix products: 107 us -> 10.7 us  [dot(): lax.dot_general(lhs, rhs, (dims, ((), ())), preferred_element_type=F32)]
    pallas_call x0 -> x3, Pallas kernels: none -> 81.8 us  [the longest x1 39.3 us: joint_backward(): pl.pallas_call(backward_kernel, grid=(N_UTT // U_STEP,), in_specs=[pl.Blo...]
    select_n x229 -> x0, other arithmetic: 29.4 us -> none  [the longest x96 19.6 us: frame_step(): terms = jnp.where(upos_ok, carry + blank_t + cum_t, NEG_FILL)]
    add x122 -> x0, other arithmetic: 19.3 us -> none  [the longest x96 17.9 us: frame_step(): return (alpha_t + blank_t, alpha_t)]
    reduce_sum x2 -> x0, other arithmetic: 18.1 us -> none  [the longest x1 17.8 us: joint_forward(): log_norm = jax.nn.logsumexp(logits, axis=-1)]
    ppermute x6 -> x0, starting transfers between devices: 14.3 us -> none  [the longest x3 10.4 us: alpha_hop(): received = lax.ppermute(row_out, 'seq', to_right)]
    ppermute x6 -> x0, waiting for transfers between devices: 12.7 us -> none  [the longest x3 10.3 us: beta_hop(): received = lax.ppermute(row_out, 'seq', to_left)]
  transfers between devices with their start and end apart: 8 -> 2, of which waited for: 8 -> 2; matrix products, arithmetic and copies ran while one was open for 2% -> 4% of each run, Pallas kernels for 0% -> 0%
where the time goes in v1:
time: 281 us
  waiting for transfers between devices  116 us (41%)
  Pallas kernels  81.8 us (29%)
  blocking collectives  40.7 us (14%)
  local copies, waits for them, and re-layouts  17.1 us (6%)
  between operations  14.1 us (5%)
  matrix products  10.7 us (4%)
    psum x1, waiting for transfers between devices, body(): grad_w_pred = lax.psum(grad_w_pred, 'data')  67.7 us
    psum x1, waiting for transfers between devices, body(): grad_w_enc = lax.psum(grad_w_enc, ('data', 'seq'))  48.3 us
    psum x1, blocking collectives, body(): dc = lax.psum(dc, 'seq').astype(BF16).reshape(N_UTT * N_UP, -1)  40.7 us
    pallas_call x1, Pallas kernels, joint_backward(): pl.pallas_call(backward_kernel, grid=(N_UTT // U_STEP,), in_specs=[pl.Blo...  39.3 us
    pallas_call x1, Pallas kernels, joint_forward(): pl.pallas_call(forward_kernel, grid=(N_UTT,), in_specs=[full(enc.shape),...  31.1 us
    unnamed x14, local copies, waits for them, and re-layouts  11.5 us
    pallas_call x1, Pallas kernels, lattice(): pl.pallas_call(lattice_kernel, in_specs=[vm] * 4, out_specs=[vm] * 4, out...  11.4 us
    dot_general x4, matrix products, dot(): lax.dot_general(lhs, rhs, (dims, ((), ())), preferred_element_type=F32)  10.7 us
  transfers between devices with their start and end apart: 2, of which 2 were waited for; matrix products, arithmetic and copies ran while one was open for 4% of the time, Pallas kernels for 0%

profile of v1, /device:TPU:0, one launch (start us, length us, event | category | flops | bytes accessed | tf_op | source)
XLA Modules:
  0.0 280.5 jit_solution(11173654331914890810)
XLA Ops:
  7.2 0.0 all-reduce.8.cloned.1.call-start
  7.2 0.7 concatenate.3
  7.9 0.1 broadcast_in_dim.21
  8.0 0.7 tile.4
  8.7 0.1 broadcast_in_dim.23
  8.7 0.7 tile.5
  9.4 0.1 broadcast_in_dim.25
  9.5 2.4 copy.14
  11.9 0.8 broadcast_in_dim.22.lab
  12.7 31.1 %joint_forward.1 = (f32[16,3,192,1024]{3,2,1,0:T(8,128)}, bf16[16,3,192,640]{3,2,1,0:T(8,128)(2,1)}, f32[18,8,128]{2,1,0:T(8,128)}, f32[72,8,128]{2,1,0:T(8,128)}) custom-call(bf16[384,1024]{1,0:T(8,128)(2,1)} %bitcast.26, bf16[384,1024]{1,0:T(8,128)(2,1)} %bitcast.27, bf16[1024,640]{1,0:T(8,128)(2,1)} %w_enc.1, bf16[1024,640]{1,0:T(8,128)(2,1)} %w_pred.1, ...), custom_call_target="tpu_custom_call" | custom-call | tf_op jit(solution)/shard_map/joint_forward/pallas_call | solution.py:76
  43.8 0.6 broadcast_in_dim.24.flen
  44.4 0.6 broadcast_in_dim.26.llen
  44.9 11.4 %lattice.1 = (f32[72,8,128]{2,1,0:T(8,128)}, f32[72,8,128]{2,1,0:T(8,128)}, f32[72,8,128]{2,1,0:T(8,128)}, f32[8,128]{1,0:T(8,128)}) custom-call(f32[18,8,128]{2,1,0:T(8,128)} %get-tuple-element.17.stat, f32[72,8,128]{2,1,0:T(8,128)} %get-tuple-element.18.sums, s32[8,128]{1,0:T(8,128)} %broadcast_in_dim.24.flen, s32[8,128]{1,0:T(8,128)} %broadcast_in_dim.26.llen), custom_call_target="tpu_custom_call" | custom-call | tf_op jit(solution)/shard_map/lattice/pallas_call | solution.py:196
  56.4 39.3 %joint_backward.1 = (bf16[16,24,640]{2,1,0:T(8,128)(2,1)}, f32[16,24,640]{2,1,0:T(8,128)}, f32[640,1024]{1,0:T(8,128)}) custom-call(f32[16,3,192,1024]{3,2,1,0:T(8,128)} %get-tuple-element.20.e_ref, bf16[16,3,192,640]{3,2,1,0:T(8,128)(2,1)} %get-tuple-element.21.h_ref, f32[72,8,128]{2,1,0:T(8,128)} %get-tuple-element.22.q0_ref, ...), custom_call_target="tpu_custom_call" | custom-call | tf_op jit(solution)/shard_map/joint_backward/pallas_call | solution.py:252
  95.7 3.7 %convolution_bitcast_fusion.1 = f32[1024,640]{0,1:T(8,128)} fusion(bf16[16,24,640]{2,1,0:T(8,128)(2,1)} %get-tuple-element.25, bf16[16,24,1024]{2,1,0:T(8,128)(2,1)} %param.8), kind=kOutput, calls=%fused_computation.1 | convolution fusion | flops 503316480 | bytes 3899392 | tf_op jit(solution)/shard_map/dot_general | solution.py:28
  99.3 0.0 copy-start.3
  99.3 0.0 copy-start.4
  99.3 0.0 all-reduce.8.cloned.1.call-update
  99.3 0.0 all-reduce.6.cloned.1.call-start
  99.4 1.1 copy-done.3
  100.5 40.7 %all-reduce.9 = bf16[16,24,640]{2,1,0:T(8,128)(2,1)S(1)} all-reduce(f32[16,24,640]{2,1,0:T(8,128)S(1)} %copy-done.3), channel_id=1, replica_groups=mesh['part'=1,'data'=2,'seq'=4] {'seq'}, use_global_device_ids=true, to_apply=%region_0.0 | all-reduce | flops 245760 | bytes 1474560 | tf_op jit(solution)/shard_map/psum | solution.py:297
  141.2 0.0 copy-done.4
  141.2 2.4 convolution_bitcast_fusion
  143.6 0.0 copy-start.2
  143.6 0.0 copy-start
  143.6 0.0 all-reduce.6.cloned.1.call-update
  143.7 1.3 slice_bitcast_fusion
  145.0 0.0 copy-done.2
  145.0 2.7 convolution_convert_fusion
  147.7 0.0 copy-done
  147.7 2.0 fusion
  149.7 48.3 %all-reduce.8.cloned.1.call-done = (f32[1024,640]{0,1:T(8,128)}, f32[640,1024]{1,0:T(8,128)}) async-done(((f32[1024,640]{0,1:T(8,128)}, f32[640,1024]{1,0:T(8,128)}), (f32[1024,640]{0,1:T(8,128)}, f32[640,1024]{1,0:T(8,128)})) %all-reduce.8.cloned.1.call-update) | async-done | bytes 5242896 | tf_op jit(solution)/shard_map/psum | solution.py:300
  198.0 3.2 %copy.15 = f32[1024,640]{1,0:T(8,128)} copy(f32[1024,640]{0,1:T(8,128)} %get-tuple-element.34) | data formatting | bytes 5242880
  201.2 0.0 copy-start.1
  201.2 67.7 %all-reduce.6.cloned.1.call-done = f32[1024,640]{0,1:T(8,128)} async-done(((f32[1024,640]{0,1:T(8,128)}), f32[1024,640]{0,1:T(8,128)}) %all-reduce.6.cloned.1.call-update) | async-done | bytes 2621456 | tf_op jit(solution)/shard_map/psum | solution.py:302
  269.0 3.2 %copy.16 = f32[1024,640]{1,0:T(8,128)} copy(f32[1024,640]{0,1:T(8,128)} %all-reduce.6.cloned.1.call-done) | data formatting | bytes 5242880
  272.2 0.0 copy-done.1
  272.2 1.5 copy.22
Async XLA Ops:
  7.2 190.9 %all-reduce.8.cloned.1.call-start = ((), (), s32[]{:S(2)}) async-start(), calls=%async_computation.1 | async-start | bytes 10485760 | tf_op jit(solution)/shard_map/psum | solution.py:300
  99.3 1.2 copy-start.3
  99.3 41.9 %copy-start.4 = (bf16[16,24,1024]{2,1,0:T(8,128)(2,1)S(1)}, bf16[16,24,1024]{2,1,0:T(8,128)(2,1)}, u32[]{:S(2)}) copy-start(bf16[16,24,1024]{2,1,0:T(8,128)(2,1)} %param.9) | copy-start | bytes 2359300
  99.3 169.6 %all-reduce.6.cloned.1.call-start = ((), (), s32[]{:S(2)}) async-start(), calls=%async_computation | async-start | bytes 5242880 | tf_op jit(solution)/shard_map/psum | solution.py:302
  143.6 1.4 copy-start.2
  143.6 4.1 %copy-start = (bf16[1024,640]{1,0:T(8,128)(2,1)S(1)}, bf16[1024,640]{1,0:T(8,128)(2,1)}, u32[]{:S(2)}) copy-start(bf16[1024,640]{1,0:T(8,128)(2,1)} %w_pred.1) | copy-start | bytes 3932164
  201.2 70.9 %copy-start.1 = (f32[640,1024]{1,0:T(8,128)S(1)}, f32[640,1024]{1,0:T(8,128)}, u32[]{:S(2)}) copy-start(f32[640,1024]{1,0:T(8,128)} %get-tuple-element.41) | copy-start | bytes 7864324
Sparse Core Ops, SparseCore 0:
  99.5 98.5 all-reduce.7
  200.3 68.6 all-reduce.5

commit v2 on v1

--- a/solution.py
+++ b/solution.py
@@ -208,7 +208,7 @@
 U_STEP = 4
 
 
-def backward_kernel(e_ref, h_ref, q0_ref, q1_ref, r_ref, lab, w_out_t, da_out, dc_out, dw_out, dz_scr):
+def backward_kernel(e_ref, h_ref, q0_ref, q1_ref, r_ref, lab, w_out_t, enc, da_out, dc_out, dw_out, dz_scr, da_all):
     step = pl.program_id(0)
     lane = lax.broadcasted_iota(jnp.int32, (8, 128), 1)
     n_v = w_out_t.shape[0]
@@ -234,19 +234,25 @@
             ds = (dh * (1.0 - hid * hid)).reshape(T_LOC, 8, n_j)
             dc_out[i, ug * 8:ug * 8 + 8, :] = jnp.sum(ds, axis=0)
             acc = ds if acc is None else acc + ds
-        da_out[i] = jnp.sum(acc, axis=1).astype(BF16)
+        da = jnp.sum(acc, axis=1).astype(BF16)
+        da_out[i] = da
+        da_all[pl.ds(pl.multiple_of(step * U_STEP * T_LOC, 16) + i * T_LOC, T_LOC), :] = da.astype(F32)
     part = dot(h_ref[...].reshape(U_STEP * UG * ROWS, n_j), dz_scr[...], ((0,), (0,)))
 
     @pl.when(step == 0)
     def _():
-        dw_out[...] = part
+        dw_out[n_j:, :] = part
 
     @pl.when(step > 0)
     def _():
-        dw_out[...] += part
-
-
-def joint_backward(e, h, q0, q1, r, lab, w_out_t):
+        dw_out[n_j:, :] += part
+
+    @pl.when(step == pl.num_programs(0) - 1)
+    def _():
+        dw_out[:n_j, :] = dot(da_all[...].astype(BF16), enc[...], ((0,), (0,)))
+
+
+def joint_backward(e, h, q0, q1, r, lab, w_out_t, enc):
     n_v, n_j = w_out_t.shape
     full = lambda shape: pl.BlockSpec(shape, lambda i: (0,) * len(shape), pipeline_mode=pl.Buffered(1))
     return pl.pallas_call(
@@ -255,22 +261,238 @@
         in_specs=[
             pl.BlockSpec((U_STEP, UG, ROWS, n_v), lambda i: (i, 0, 0, 0)),
             pl.BlockSpec((U_STEP, UG, ROWS, n_j), lambda i: (i, 0, 0, 0)),
-            full(q0.shape), full(q1.shape), full(r.shape), full(lab.shape), full(w_out_t.shape),
+            full(q0.shape), full(q1.shape), full(r.shape), full(lab.shape), full(w_out_t.shape), full(enc.shape),
         ],
         out_specs=[
             pl.BlockSpec((U_STEP, T_LOC, n_j), lambda i: (i, 0, 0)),
             pl.BlockSpec((U_STEP, N_UP, n_j), lambda i: (i, 0, 0)),
-            pl.BlockSpec((n_j, n_v), lambda i: (0, 0)),
+            pl.BlockSpec((2 * n_j, n_v), lambda i: (0, 0)),
         ],
         out_shape=[
             jax.ShapeDtypeStruct((N_UTT, T_LOC, n_j), BF16),
             jax.ShapeDtypeStruct((N_UTT, N_UP, n_j), F32),
-            jax.ShapeDtypeStruct((n_j, n_v), F32),
+            jax.ShapeDtypeStruct((2 * n_j, n_v), F32),
         ],
-        scratch_shapes=[pltpu.VMEM((U_STEP * UG * ROWS, n_v), BF16)],
+        scratch_shapes=[pltpu.VMEM((U_STEP * UG * ROWS, n_v), BF16), pltpu.VMEM((N_UTT * T_LOC, n_j), F32)],
         compiler_params=pltpu.CompilerParams(vmem_limit_bytes=VMEM_FULL),
         name="joint_backward",
-    )(e, h, q0, q1, r, lab, w_out_t)
+    )(e, h, q0, q1, r, lab, w_out_t, enc)
+
+
+class Links:
+    def __init__(self, send_sem, recv_sem):
+        self.send_sem, self.recv_sem, self.used, self.copies = send_sem, recv_sem, 0, []
+        seq = lax.axis_index("seq")
+        self.core = lax.rem(seq, 2)
+        self.x = lax.div(seq, 2)
+        self.y = lax.axis_index("data")
+        self.seq = seq
+        self.dev = {
+            "core": {"seq": seq + 1 - 2 * self.core},
+            "x": {"seq": lax.rem(seq + 2, N_SEQ)},
+            "y": {"data": 1 - self.y},
+        }
+
+    def greet(self):
+        barrier = pltpu.get_barrier_semaphore()
+        for dev in self.dev.values():
+            pl.semaphore_signal(barrier, inc=1, device_id=dev, device_id_type=MESH)
+        pl.semaphore_wait(barrier, 3)
+
+    def send(self, src, dst, axis):
+        i = self.used
+        self.used += 1
+        cp = pltpu.make_async_remote_copy(src_ref=src, dst_ref=dst, send_sem=self.send_sem.at[i], recv_sem=self.recv_sem.at[i],
+                                          device_id=self.dev[axis], device_id_type=MESH)
+        cp.start()
+        self.copies.append(cp)
+        return cp
+
+
+def rows_at(start, size):
+    return pl.ds(pl.multiple_of(start, 16), size)
+
+
+def sum_stages(links, src, acc, gat, stg, rcv):
+    n_row, n_col = src.shape
+    half = n_row // 2
+    h0 = links.core * half
+    box = []
+    for q in range(2):
+        first, second = ("x", "y") if q == 0 else ("y", "x")
+        k1, k2 = (links.x, links.y) if q == 0 else (links.y, links.x)
+        box.append((first, second, k1, k2, h0, half, pl.ds(q * (n_col // 2), n_col // 2)))
+    live = {}
+
+    def s1():
+        stg[0][...] = src[rows_at((1 - links.core) * half, half), :].astype(BF16)
+        live["c"] = links.send(stg[0], rcv[0], "core")
+
+    def s2():
+        live["c"].wait_recv()
+        acc[...] = src[rows_at(h0, half), :] + rcv[0][...].astype(F32)
+        for q, (first, second, k1, k2, base, n, cols) in enumerate(box):
+            stg[1][q] = acc[rows_at((1 - k1) * (n // 2), n // 2), cols].astype(BF16)
+            live[q] = links.send(stg[1].at[q], rcv[1].at[q], first)
+
+    def s3():
+        for q, (first, second, k1, k2, base, n, cols) in enumerate(box):
+            live[q].wait_recv()
+            part = rows_at((1 - k2) * (n // 4), n // 4)
+            stg[2][q] = (acc[rows_at(k1 * (n // 2) + (1 - k2) * (n // 4), n // 4), cols] + rcv[1][q, part].astype(F32)).astype(BF16)
+            live[q] = links.send(stg[2].at[q], rcv[2].at[q], second)
+
+    def s4():
+        for q, (first, second, k1, k2, base, n, cols) in enumerate(box):
+            live[q].wait_recv()
+            own = rows_at(base + k1 * (n // 2) + k2 * (n // 4), n // 4)
+            part = rows_at(k2 * (n // 4), n // 4)
+            total = acc[rows_at(k1 * (n // 2) + k2 * (n // 4), n // 4), cols] + rcv[1][q, part].astype(F32) + rcv[2][q].astype(F32)
+            gat[own, cols] = total.astype(BF16)
+            live[q] = links.send(gat.at[own, cols], gat.at[own, cols], second)
+
+    def s5():
+        for q, (first, second, k1, k2, base, n, cols) in enumerate(box):
+            live[q].wait_recv()
+            own = rows_at(base + k1 * (n // 2), n // 2)
+            live[q] = links.send(gat.at[own, cols], gat.at[own, cols], first)
+
+    def s6():
+        for q in range(2):
+            live[q].wait_recv()
+        own = rows_at(h0, half)
+        live["c"] = links.send(gat.at[own, :], gat.at[own, :], "core")
+
+    def s7():
+        live["c"].wait_recv()
+
+    return [s1, s2, s3, s4, s5, s6, s7]
+
+
+def dc_stages(links, src, gat, stg, rcv):
+    n_row, n_col = src.shape
+    half, quar = n_row // 2, n_row // 4
+    h0 = links.core * half
+    r0 = h0 + links.x * quar
+    live = {}
+
+    def s1():
+        stg[0][...] = src[rows_at((1 - links.core) * half, half), :].astype(BF16)
+        live["c"] = links.send(stg[0], rcv[0], "core")
+
+    def s2():
+        live["c"].wait_recv()
+        part = rows_at((1 - links.x) * quar, quar)
+        stg[1][...] = (src[rows_at(h0 + (1 - links.x) * quar, quar), :] + rcv[0][part, :].astype(F32)).astype(BF16)
+        live["x"] = links.send(stg[1], rcv[1], "x")
+
+    y_own, y_far = links.y * n_row, (1 - links.y) * n_row
+
+    def hop(start, size, axis):
+        rows = rows_at(start, size)
+        return links.send(gat.at[rows, :], gat.at[rows, :], axis)
+
+    def s3():
+        live["x"].wait_recv()
+        part = rows_at(links.x * quar, quar)
+        total = src[rows_at(r0, quar), :] + rcv[0][part, :].astype(F32) + rcv[1][...].astype(F32)
+        gat[rows_at(y_own + r0, quar), :] = total.astype(BF16)
+        live["y"] = hop(y_own + r0, quar, "y")
+
+    def s4():
+        live["own"] = hop(y_own + r0, quar, "x")
+        live["y"].wait_recv()
+        live["far"] = hop(y_far + r0, quar, "x")
+
+    def s5():
+        live["own"].wait_recv()
+        live["own"] = hop(y_own + h0, half, "core")
+        live["far"].wait_recv()
+        live["far"] = hop(y_far + h0, half, "core")
+
+    def s6():
+        live["own"].wait_recv()
+        live["far"].wait_recv()
+
+    return [s1, s2, s3, s4, s5, s6]
+
+
+N_COPY = 10 + 7
+
+
+def exchange_kernel(dw, dc, g_w, g_dc, acc_w, ws0, ws1, ws2, wr0, wr1, wr2, ds0, ds1, dr0, dr1, send_sem, recv_sem):
+    links = Links(send_sem, recv_sem)
+    links.greet()
+    st_w = sum_stages(links, dw, acc_w, g_w, (ws0, ws1, ws2), (wr0, wr1, wr2))
+    st_dc = dc_stages(links, dc, g_dc, (ds0, ds1), (dr0, dr1))
+    for i in range(7):
+        for stages in (st_dc, st_w):
+            if i < len(stages):
+                stages[i]()
+    for cp in links.copies:
+        cp.wait_send()
+
+
+def sum_scratch(n_row, n_col):
+    half = n_row // 2
+    return [pltpu.VMEM((half, n_col), BF16), pltpu.VMEM((2, half // 2, n_col // 2), BF16), pltpu.VMEM((2, half // 4, n_col // 2), BF16)]
+
+
+def exchange(dw, dc):
+    n_r, n_j = dc.shape
+    vm = pl.BlockSpec(memory_space=pltpu.VMEM)
+    dc_bufs = [pltpu.VMEM((n_r // 2, n_j), BF16), pltpu.VMEM((n_r // 4, n_j), BF16)]
+    return pl.pallas_call(
+        exchange_kernel,
+        in_specs=[vm] * 2,
+        out_specs=[vm] * 2,
+        out_shape=[jax.ShapeDtypeStruct(dw.shape, BF16), jax.ShapeDtypeStruct((2 * n_r, n_j), BF16)],
+        scratch_shapes=[pltpu.VMEM((dw.shape[0] // 2, dw.shape[1]), F32)] + sum_scratch(*dw.shape) * 2 + dc_bufs * 2
+        + [pltpu.SemaphoreType.DMA((N_COPY,)), pltpu.SemaphoreType.DMA((N_COPY,))],
+        compiler_params=pltpu.CompilerParams(collective_id=1, has_side_effects=True, vmem_limit_bytes=VMEM_FULL),
+        name="exchange",
+    )(dw, dc)
+
+
+def finish_kernel(g_w, g_dc, pred, pred_far, w_pred, da, w_enc, o_enc, o_pred, o_wenc, o_wpred, o_wout,
+                  v_enc, v_pred, v_wenc, v_wpred, v_wout, sem):
+    y = lax.axis_index("data")
+    jobs = []
+
+    def put(src, dst, i):
+        cp = pltpu.make_async_copy(src, dst, sem.at[i])
+        cp.start()
+        jobs.append(cp)
+
+    n_j = w_pred.shape[1]
+    v_wenc[...] = g_w[:n_j, :].astype(F32).T
+    put(v_wenc, o_wenc, 0)
+    v_wout[...] = g_w[n_j:, :].astype(F32)
+    put(v_wout, o_wout, 1)
+    n_r = pred.shape[0]
+    dc_own, dc_far = g_dc[rows_at(y * n_r, n_r), :], g_dc[rows_at((1 - y) * n_r, n_r), :]
+    v_wpred[...] = dot(pred[...], dc_own, ((0,), (0,))) + dot(pred_far[...], dc_far, ((0,), (0,)))
+    put(v_wpred, o_wpred, 2)
+    v_pred[...] = dot(dc_own, w_pred[...], ((1,), (1,)))
+    put(v_pred, o_pred, 3)
+    v_enc[...] = dot(da[...], w_enc[...], ((1,), (1,))).astype(BF16)
+    put(v_enc, o_enc, 4)
+    for cp in jobs:
+        cp.wait()
+
+
+def finish(g_w, g_dc, pred, pred_far, w_pred, da, w_enc):
+    vm = pl.BlockSpec(memory_space=pltpu.VMEM)
+    outs = [(pred.shape, BF16), (pred.shape, F32), (w_pred.shape, F32), (w_pred.shape, F32), (w_pred.shape[::-1], F32)]
+    return pl.pallas_call(
+        finish_kernel,
+        in_specs=[vm] * 7,
+        out_specs=[pl.BlockSpec(memory_space=pl.ANY)] * 5,
+        out_shape=[jax.ShapeDtypeStruct(*o) for o in outs],
+        scratch_shapes=[pltpu.VMEM(*o) for o in outs] + [pltpu.SemaphoreType.DMA((5,))],
+        compiler_params=pltpu.CompilerParams(vmem_limit_bytes=VMEM_FULL),
+        name="finish",
+    )(g_w, g_dc, pred, pred_far, w_pred, da, w_enc)
 
 
 def solution(mesh):
@@ -287,19 +509,14 @@
         lab = jnp.broadcast_to(lab_ids.reshape(N_UTT * N_UP, 1), (N_UTT * N_UP, 128))
         enc2 = enc_loc.reshape(N_UTT * T_LOC, n_h)
         pred2 = pred_loc.reshape(N_UTT * N_UP, n_h)
+        pred_far = lax.ppermute(pred2, "data", [(0, 1), (1, 0)])
         e, h, stat, sums = joint_forward(enc2, pred2, w_enc, w_pred, w_out, lab)
         lens = lambda v: jnp.broadcast_to(jnp.tile(v, 8)[None], (8, 128))
         q0, q1, r, loss = lattice(stat, sums, lens(frame_len), lens(label_len))
-        da, dc, grad_w_out = joint_backward(e, h, q0, q1, r, lab, w_out.T)
+        da, dc, dw = joint_backward(e, h, q0, q1, r, lab, w_out.T, enc2)
         da2 = da.reshape(N_UTT * T_LOC, -1)
-        grad_enc = dot(da2, w_enc, ((1,), (1,))).astype(BF16).reshape(enc_loc.shape)
-        grad_w_enc = dot(enc2, da2, ((0,), (0,)))
-        dc = lax.psum(dc, "seq").astype(BF16).reshape(N_UTT * N_UP, -1)
-        grad_pred = dot(dc, w_pred, ((1,), (1,))).reshape(pred_loc.shape)
-        grad_w_pred = dot(pred2, dc, ((0,), (0,)))
-        grad_w_enc = lax.psum(grad_w_enc, ("data", "seq"))
-        grad_w_out = lax.psum(grad_w_out, ("data", "seq"))
-        grad_w_pred = lax.psum(grad_w_pred, "data")
-        return loss[0, :N_UTT], grad_enc, grad_pred, grad_w_enc, grad_w_pred, grad_w_out
+        g_w, g_dc = exchange(dw, dc.reshape(N_UTT * N_UP, -1))
+        grad_enc, grad_pred, grad_w_enc, grad_w_pred, grad_w_out = finish(g_w, g_dc, pred2, pred_far, w_pred, da2, w_enc)
+        return loss[0, :N_UTT], grad_enc.reshape(enc_loc.shape), grad_pred.reshape(pred_loc.shape), grad_w_enc, grad_w_pred, grad_w_out
 
     return jax.shard_map(body, mesh=mesh, in_specs=(enc_spec, utt_cube, weight_in, weight_in, weight_in, utt_mats, utt_rows, utt_rows), out_specs=(utt_rows, enc_spec, utt_cube, weight_out, weight_out, weight_out), check_vma=False)

time: 281 us -> 149 us (0.53)
  waiting for transfers between devices: 116 us -> 0.01 us
  Pallas kernels: 81.8 us -> 137 us
  blocking collectives: 40.7 us -> 0 us
  between operations: 14.1 us -> 0.82 us
  matrix products: 10.7 us -> 0 us
  local copies, waits for them, and re-layouts: 17.1 us -> 7.85 us
  starting transfers between devices: 0.08 us -> 3.39 us
    psum x2 -> x0, waiting for transfers between devices: 116 us -> none  [the longest x1 67.7 us: body(): grad_w_pred = lax.psum(grad_w_pred, 'data')]
    pallas_call x0 -> x2, Pallas kernels: none -> 53.7 us  [the longest x1 43.5 us: exchange(): pl.pallas_call(exchange_kernel, in_specs=[vm] * 2, out_specs=[vm] * 2, ou...]
    psum x1 -> x0, blocking collectives: 40.7 us -> none  [body(): dc = lax.psum(dc, 'seq').astype(BF16).reshape(N_UTT * N_UP, -1)]
    dot_general x4 -> x0, matrix products: 10.7 us -> none  [dot(): lax.dot_general(lhs, rhs, (dims, ((), ())), preferred_element_type=F32)]
    unnamed x14 -> x1, local copies, waits for them, and re-layouts: 11.5 us -> 2.42 us
    ppermute x0 -> x1, starting transfers between devices: none -> 3.39 us  [body(): pred_far = lax.ppermute(pred2, 'data', [(0, 1), (1, 0)])]
  transfers between devices with their start and end apart: 2 -> 1, of which waited for: 2 -> 0; matrix products, arithmetic and copies ran while one was open for 4% -> 5% of each run, Pallas kernels for 0% -> 85%
where the time goes in v2:
time: 149 us
  Pallas kernels  137 us (92%)
  local copies, waits for them, and re-layouts  7.85 us (5%)
  starting transfers between devices  3.39 us (2%)
    pallas_call x1, Pallas kernels, exchange(): pl.pallas_call(exchange_kernel, in_specs=[vm] * 2, out_specs=[vm] * 2, ou...  43.5 us
    pallas_call x1, Pallas kernels, joint_backward(): pl.pallas_call(backward_kernel, grid=(N_UTT // U_STEP,), in_specs=[pl.Blo...  41.8 us
    pallas_call x1, Pallas kernels, joint_forward(): pl.pallas_call(forward_kernel, grid=(N_UTT,), in_specs=[full(enc.shape),...  31 us
    pallas_call x1, Pallas kernels, finish(): pl.pallas_call(finish_kernel, in_specs=[vm] * 7, out_specs=[pl.BlockSpec(...  10.3 us
    pallas_call x1, Pallas kernels, lattice(): pl.pallas_call(lattice_kernel, in_specs=[vm] * 4, out_specs=[vm] * 4, out...  10.1 us
    ppermute x1, starting transfers between devices, body(): pred_far = lax.ppermute(pred2, 'data', [(0, 1), (1, 0)])  3.39 us
  transfers between devices with their start and end apart: 1, of which 0 were waited for; matrix products, arithmetic and copies ran while one was open for 5% of the time, Pallas kernels for 85%

profile of v2, /device:TPU:0, one launch (start us, length us, event | category | flops | bytes accessed | tf_op | source)
XLA Modules:
  0.0 148.7 jit_solution(13665724921765299227)
XLA Ops:
  0.6 3.4 %collective-permute-start = (bf16[384,1024]{1,0:T(8,128)(2,1)}, bf16[384,1024]{1,0:T(8,128)(2,1)}, u32[]{:S(2)}, u32[]{:S(2)}) collective-permute-start(bf16[384,1024]{1,0:T(8,128)(2,1)} %bitcast.12), channel_id=1, source_target_pairs={{0,4},{4,0},{1,5},{5,1},{2,6},{6,2},{3,7},{7,3}} | collective-permute-start | bytes 2359304 | tf_op jit(solution)/shard_map/ppermute | solution.py:512
  4.0 0.7 concatenate.3
  4.7 0.1 broadcast_in_dim.21
  4.8 0.7 tile.4
  5.5 0.1 broadcast_in_dim.23
  5.6 0.7 tile.5
  6.2 0.1 broadcast_in_dim.25
  6.3 2.4 %copy.14 = bf16[640,1024]{0,1:T(8,128)(2,1)} copy(bf16[640,1024]{1,0:T(8,128)(2,1)} %w_out.1) | data formatting | bytes 2621440 | tf_op args[4]
  8.7 0.8 broadcast_in_dim.22.lab
  9.5 31.0 %joint_forward.1 = (f32[16,3,192,1024]{3,2,1,0:T(8,128)}, bf16[16,3,192,640]{3,2,1,0:T(8,128)(2,1)}, f32[18,8,128]{2,1,0:T(8,128)}, f32[72,8,128]{2,1,0:T(8,128)}) custom-call(bf16[384,1024]{1,0:T(8,128)(2,1)} %bitcast.10, bf16[384,1024]{1,0:T(8,128)(2,1)} %bitcast.13, bf16[1024,640]{1,0:T(8,128)(2,1)} %w_enc.3, bf16[1024,640]{1,0:T(8,128)(2,1)} %w_pred.3, ...), custom_call_target="tpu_custom_call" | custom-call | tf_op jit(solution)/shard_map/joint_forward/pallas_call | solution.py:76
  40.6 0.6 broadcast_in_dim.24.flen
  41.2 0.6 broadcast_in_dim.26.llen
  41.7 10.1 %lattice.1 = (f32[72,8,128]{2,1,0:T(8,128)}, f32[72,8,128]{2,1,0:T(8,128)}, f32[72,8,128]{2,1,0:T(8,128)}, f32[8,128]{1,0:T(8,128)}) custom-call(f32[18,8,128]{2,1,0:T(8,128)} %get-tuple-element.24.stat, f32[72,8,128]{2,1,0:T(8,128)} %get-tuple-element.25.sums, s32[8,128]{1,0:T(8,128)} %broadcast_in_dim.24.flen, s32[8,128]{1,0:T(8,128)} %broadcast_in_dim.26.llen), custom_call_target="tpu_custom_call" | custom-call | tf_op jit(solution)/shard_map/lattice/pallas_call | solution.py:196
  51.9 41.8 %joint_backward.1 = (bf16[16,24,640]{2,1,0:T(8,128)(2,1)}, f32[16,24,640]{2,1,0:T(8,128)}, f32[1280,1024]{1,0:T(8,128)}) custom-call(f32[16,3,192,1024]{3,2,1,0:T(8,128)} %get-tuple-element.27.e_ref, bf16[16,3,192,640]{3,2,1,0:T(8,128)(2,1)} %get-tuple-element.28.h_ref, f32[72,8,128]{2,1,0:T(8,128)} %get-tuple-element.29.q0_ref, ...), custom_call_target="tpu_custom_call" | custom-call | tf_op jit(solution)/shard_map/joint_backward/pallas_call | solution.py:258
  93.6 43.5 %exchange.1 = (bf16[1280,1024]{1,0:T(8,128)(2,1)}, bf16[768,640]{1,0:T(8,128)(2,1)}) custom-call(f32[1280,1024]{1,0:T(8,128)} %get-tuple-element.32.dw, f32[384,640]{1,0:T(8,128)} %bitcast.15), custom_call_target="tpu_custom_call" | custom-call | tf_op jit(solution)/shard_map/exchange/pallas_call | solution.py:445
  137.1 1.2 slice_bitcast_fusion
  138.3 0.0 collective-permute-done.pred_far
  138.3 10.3 %finish.1 = (bf16[384,1024]{1,0:T(8,128)(2,1)}, f32[384,1024]{1,0:T(8,128)}, f32[1024,640]{1,0:T(8,128)}, f32[1024,640]{1,0:T(8,128)}, f32[640,1024]{1,0:T(8,128)}) custom-call(bf16[1280,1024]{1,0:T(8,128)(2,1)} %get-tuple-element.34.g_w, bf16[768,640]{1,0:T(8,128)(2,1)} %get-tuple-element.35.g_dc, bf16[384,1024]{1,0:T(8,128)(2,1)} %bitcast.14, ...), custom_call_target="tpu_custom_call" | custom-call | tf_op jit(solution)/shard_map/finish/pallas_call | solution.py:487
Async XLA Ops:
  0.6 137.7 %collective-permute-start = (bf16[384,1024]{1,0:T(8,128)(2,1)}, bf16[384,1024]{1,0:T(8,128)(2,1)}, u32[]{:S(2)}, u32[]{:S(2)}) collective-permute-start(bf16[384,1024]{1,0:T(8,128)(2,1)} %bitcast.12), channel_id=1, source_target_pairs={{0,4},{4,0},{1,5},{5,1},{2,6},{6,2},{3,7},{7,3}} | collective-permute-start | bytes 2359304 | tf_op jit(solution)/shard_map/ppermute | solution.py:512

commit v3 on v1

v3 whole, which is shorter than its diff:
```python
import functools

import jax
import jax.numpy as jnp
from jax import lax
from jax.experimental import pallas as pl
from jax.experimental.pallas import tpu as pltpu
from jax.sharding import PartitionSpec as P

NEG = -1e30
SUB = 8
LANES = 128
LOG2E = 1.4426950408889634
LN2 = 0.6931471805599453
F32 = jnp.float32
BF16 = jnp.bfloat16
MESH = pl.DeviceIdType.MESH
VMEM_FULL = 67_000_000
N_UTT = 16
T_LOC = 24
N_UP = 24
UG = 3
N_SEQ = 4
T_ALL = T_LOC * N_SEQ
RING = 4
N_DIAG = T_ALL + N_UP - 1
ROWS = SUB * T_LOC


def dot(lhs, rhs, dims=((1,), (0,))):
    return lax.dot_general(lhs, rhs, (dims, ((), ())), preferred_element_type=F32)


def label_column(labels, utt, ug, sub):
    col = jnp.zeros((SUB, LANES), jnp.int32)
    for k in range(SUB):
        if ug * SUB + k < N_UP - 1:
            col = jnp.where(sub == k, labels[utt, ug * SUB + k], col)
    return col


def forward_kernel(labels, enc, pred, w_enc, w_pred, w_out, z_hbm, h_hbm, stat_out, norm_out, act_e, act_p, h_next, z_last, z_ring, h_ring, z_sem, h_sem):
    step = pl.program_id(0)
    lane = lax.broadcasted_iota(jnp.int32, (SUB, LANES), 1)
    sub = lax.broadcasted_iota(jnp.int32, (SUB, LANES), 0)
    n_v = w_out.shape[1]

    @pl.when(step == 0)
    def _():
        act_e[...] = dot(enc[...], w_enc[...]).astype(BF16).astype(F32)
        act_p[...] = dot(pred[...], w_pred[...]).astype(BF16).astype(F32)
        stat_out[...] = jnp.zeros_like(stat_out)
        norm_out[...] = jnp.zeros_like(norm_out)

    def hidden(utt, ug, dst):
        row = pl.multiple_of(utt * N_UP, SUB)
        c_grp = act_p[pl.ds(row + SUB * ug, SUB), :]
        a_utt = act_e[pl.ds(row, T_LOC), :]
        for t in range(0, T_LOC, 2):
            pre = jnp.concatenate([a_utt[t:t + 1, :] + c_grp, a_utt[t + 1:t + 2, :] + c_grp], axis=0)
            dst[t * SUB:t * SUB + 16, :] = jnp.tanh(pre).astype(BF16)

    def soften(utt, ug, src):
        lab_grp = label_column(labels, jnp.maximum(utt, 0), ug, sub)
        masks = [lab_grp - LANES * k == lane for k in range(n_v // LANES)]
        for t4 in range(T_LOC // 4):
            cur = stat_out[ug * 6 + t4]
            for k in range(4):
                t = t4 * 4 + k
                z = [src[t * SUB:t * SUB + SUB, c * LANES:c * LANES + LANES] for c in range(n_v // LANES)]
                top = functools.reduce(jnp.maximum, z)
                tot = functools.reduce(jnp.add, [jnp.exp2((v - top) * LOG2E) for v in z])
                picked = functools.reduce(jnp.add, [jnp.where(m, v, 0.0) for m, v in zip(masks, z)])
                row_top = jnp.max(top, axis=1, keepdims=True)
                row_tot = jnp.sum(tot * jnp.exp2((top - row_top) * LOG2E), axis=1, keepdims=True)
                norm = row_top * LOG2E + jnp.log2(row_tot)
                blank = z[0][:, 0:1] * LOG2E - norm
                label = jnp.sum(picked, axis=1, keepdims=True) * LOG2E - norm
                cur = jnp.where(lane == utt + 32 * k, blank, cur)
                cur = jnp.where(lane == utt + 32 * k + 16, label, cur)
                norm_out[ug * T_LOC + t] = jnp.where(lane == utt, norm, norm_out[ug * T_LOC + t])
            stat_out[ug * 6 + t4] = cur

    def puts(utt):
        at = lax.rem(utt, RING)
        return (pltpu.make_async_copy(z_ring.at[at], z_hbm.at[utt], z_sem.at[at]),
                pltpu.make_async_copy(h_ring.at[at], h_hbm.at[utt], h_sem.at[at]))

    @pl.when(step == 0)
    def _():
        hidden(0, 0, h_next)

    @pl.when(step >= RING)
    def _():
        for cp in puts(step - RING):
            cp.wait()

    slot = lax.rem(step, RING)
    z_out, h_out = z_ring.at[pl.ds(slot, 1)], h_ring.at[pl.ds(slot, 1)]
    h_out[0, 0] = h_next[...]
    z_out[0, 0] = dot(h_next[...], w_out[...])
    hidden(step, 1, h_out.at[0, 1])
    soften(step - 1, 2, z_last)
    z_out[0, 1] = dot(h_out[0, 1], w_out[...])
    hidden(step, 2, h_out.at[0, 2])
    soften(step, 0, z_out.at[0, 0])
    z_two = dot(h_out[0, 2], w_out[...])
    z_last[...] = z_two
    z_out[0, 2] = z_two
    hidden(jnp.minimum(step + 1, N_UTT - 1), 0, h_next)
    soften(step, 1, z_out.at[0, 1])
    for cp in puts(step):
        cp.start()

    @pl.when(step == N_UTT - 1)
    def _():
        soften(step, 2, z_last)
        for back in range(RING - 1, -1, -1):
            for cp in puts(step - back):
                cp.wait()


def joint_forward(labels, enc, pred, w_enc, w_pred, w_out):
    n_j, n_v = w_out.shape
    full = lambda shape: pl.BlockSpec(shape, lambda i: (0,) * len(shape), pipeline_mode=pl.Buffered(1))
    return pl.pallas_call(
        forward_kernel,
        grid=(N_UTT,),
        in_specs=[pl.BlockSpec(memory_space=pltpu.SMEM)] + [full(v.shape) for v in (enc, pred, w_enc, w_pred, w_out)],
        out_specs=[
            pl.BlockSpec(memory_space=pl.ANY),
            pl.BlockSpec(memory_space=pl.ANY),
            pl.BlockSpec((UG * 6, SUB, LANES), lambda i: (0, 0, 0)),
            pl.BlockSpec((UG * T_LOC, SUB, LANES), lambda i: (0, 0, 0)),
        ],
        out_shape=[
            jax.ShapeDtypeStruct((N_UTT, UG, ROWS, n_v), F32),
            jax.ShapeDtypeStruct((N_UTT, UG, ROWS, n_j), BF16),
            jax.ShapeDtypeStruct((UG * 6, SUB, LANES), F32),
            jax.ShapeDtypeStruct((UG * T_LOC, SUB, LANES), F32),
        ],
        scratch_shapes=[pltpu.VMEM((N_UTT * T_LOC, n_j), F32), pltpu.VMEM((N_UTT * N_UP, n_j), F32), pltpu.VMEM((ROWS, n_j), BF16), pltpu.VMEM((ROWS, n_v), F32),
            pltpu.VMEM((RING, UG, ROWS, n_v), F32), pltpu.VMEM((RING, UG, ROWS, n_j), BF16),
            pltpu.SemaphoreType.DMA((RING,)), pltpu.SemaphoreType.DMA((RING,))],
        compiler_params=pltpu.CompilerParams(vmem_limit_bytes=VMEM_FULL),
        name="joint_forward",
    )(labels, enc, pred, w_enc, w_pred, w_out)


def lae2(x, y):
    return jnp.maximum(x, y) + jnp.log2(1.0 + jnp.exp2(-jnp.abs(x - y)))


def lattice_kernel(stat, norm, flen, llen, q0_out, q1_out, norm_out, loss_out, gath, s_blank, s_label, s_alpha, s_beta, send_sem, recv_sem):
    me = lax.axis_index("seq")
    barrier = pltpu.get_barrier_semaphore()
    for off in range(1, N_SEQ):
        pl.semaphore_signal(barrier, inc=1, device_id={"seq": lax.rem(me + off, N_SEQ)}, device_id_type=MESH)
    pl.semaphore_wait(barrier, N_SEQ - 1)
    copies = []
    for off in range(1, N_SEQ):
        cp = pltpu.make_async_remote_copy(
            src_ref=stat, dst_ref=gath.at[off - 1], send_sem=send_sem.at[off - 1], recv_sem=recv_sem.at[off - 1],
            device_id={"seq": lax.rem(me + off, N_SEQ)}, device_id_type=MESH)
        cp.start()
        copies.append(cp)

    sub = lax.broadcasted_iota(jnp.int32, (SUB, LANES), 0)
    sub24 = lax.broadcasted_iota(jnp.int32, (N_UP, LANES), 0)
    lane = lax.broadcasted_iota(jnp.int32, (SUB, LANES), 1)
    tb = jnp.zeros((SUB, LANES), jnp.int32)
    ub = jnp.zeros((SUB, LANES), jnp.int32)
    for b in range(N_UTT):
        at_b = lax.rem(lane, N_UTT) == b
        tb = jnp.where(at_b, flen[b], tb)
        ub = jnp.where(at_b, llen[b], ub)
    n_pad = s_blank.shape[0]

    def fill(i, c):
        s_blank[pl.ds(pl.multiple_of(i * SUB, SUB), SUB), :] = jnp.full((SUB, LANES), NEG, F32)
        s_label[pl.ds(pl.multiple_of(i * SUB, SUB), SUB), :] = jnp.full((SUB, LANES), NEG, F32)
        return c

    lax.fori_loop(0, n_pad // SUB, fill, 0, unroll=SUB)
    end_grp = [jnp.where(sub + SUB * ug == ub, 0.0, NEG) for ug in range(UG)]
    for t in range(T_ALL, T_ALL + N_UP):
        for ug in range(UG):
            s_blank[pl.ds(t * N_UP + 200 * ug, SUB, stride=25), :] = end_grp[ug]

    def place(src, src_seq):
        for t4 in range(T_LOC // 4):
            for ug in range(UG):
                val = src[ug * 6 + t4]
                in_u = sub + SUB * ug <= ub
                in_l = sub + SUB * ug < ub
                for k in range(4):
                    t = src_seq * T_LOC + t4 * 4 + k
                    bl = val if k == 0 else pltpu.roll(val, LANES - 32 * k, 1)
                    la = pltpu.roll(val, 112 - 32 * k, 1)
                    ok = t < tb
                    s_blank[pl.ds(t * N_UP + 200 * ug, SUB, stride=25), :] = jnp.where(ok, jnp.where(in_u, bl, NEG), end_grp[ug])
                    s_label[pl.ds(t * N_UP + 200 * ug, SUB, stride=25), :] = jnp.where(ok & in_l, la, NEG)

    place(stat, me)
    for off in range(1, N_SEQ):
        copies[off - 1].wait_recv()
        place(gath.at[off - 1], lax.rem(me + N_SEQ - off, N_SEQ))

    alpha0 = jnp.where(sub24 == 0, 0.0, NEG)
    s_alpha[pl.ds(0, N_UP), :] = alpha0
    beta_end = jnp.where(sub24 == jnp.concatenate([ub] * UG, axis=0), 0.0, NEG)
    s_beta[pl.ds(N_DIAG * N_UP, N_UP), :] = beta_end
    s_beta[pl.ds((N_DIAG + 1) * N_UP, SUB), :] = jnp.full((SUB, LANES), NEG, F32)

    def wave(i, carry):
        alpha, beta = carry
        row = pl.multiple_of(i * N_UP, SUB)
        x = alpha + s_blank[pl.ds(row, N_UP), :]
        y = alpha + s_label[pl.ds(row, N_UP), :]
        y = jnp.where(sub24 == 0, NEG, pltpu.roll(y, 1, 0))
        alpha = lae2(x, y)
        s_alpha[pl.ds(pl.multiple_of(row + N_UP, SUB), N_UP), :] = alpha
        brow = pl.multiple_of((N_DIAG - 1 - i) * N_UP, SUB)
        bx = beta + s_blank[pl.ds(brow, N_UP), :]
        by = pltpu.roll(beta, N_UP - 1, 0) + s_label[pl.ds(brow, N_UP), :]
        beta = lae2(bx, by)
        s_beta[pl.ds(brow, N_UP), :] = beta
        return alpha, beta

    _, beta = lax.fori_loop(0, N_DIAG, wave, (alpha0, beta_end), unroll=7)
    log_p = beta[0:1, :]
    loss_out[...] = jnp.broadcast_to(-LN2 * log_p, (SUB, LANES))
    for t in range(T_LOC):
        tg = me * T_LOC + t
        for ug in range(UG):
            base = tg * N_UP + 200 * ug
            grp = lambda ref, off: ref[pl.ds(base + off, SUB, stride=25), :]
            al = grp(s_alpha, 0) - log_p
            ok = (tg < tb) & (sub + SUB * ug <= ub)
            q0 = jnp.where(ok, jnp.exp2(al + grp(s_blank, 0) + grp(s_beta, 24)), 0.0)
            q1 = jnp.where(ok, jnp.exp2(al + grp(s_label, 0) + grp(s_beta, 25)), 0.0)
            idx = ug * T_LOC + t
            q0_out[idx] = q0
            q1_out[idx] = q1
            norm_out[idx] = norm[idx] - jnp.log2(q0 + q1)
    for cp in copies:
        cp.wait_send()


def lattice(stat, norm, flen, llen):
    vm = pl.BlockSpec(memory_space=pltpu.VMEM)
    n_rows = (T_ALL + 2 * N_UP) * N_UP
    return pl.pallas_call(
        lattice_kernel,
        in_specs=[vm] * 2 + [pl.BlockSpec(memory_space=pltpu.SMEM)] * 2,
        out_specs=[vm] * 4,
        out_shape=[jax.ShapeDtypeStruct((UG * T_LOC, SUB, LANES), F32)] * 3 + [jax.ShapeDtypeStruct((SUB, LANES), F32)],
        scratch_shapes=[pltpu.VMEM((N_SEQ - 1,) + stat.shape, F32)] + [pltpu.VMEM((n_rows, LANES), F32)] * 4
        + [pltpu.SemaphoreType.DMA((N_SEQ - 1,)), pltpu.SemaphoreType.DMA((N_SEQ - 1,))],
        compiler_params=pltpu.CompilerParams(collective_id=0, has_side_effects=True),
        name="lattice",
    )(stat, norm, flen, llen)


class Links:
    def __init__(self, send_sem, recv_sem):
        self.send_sem, self.recv_sem, self.copies = send_sem, recv_sem, []
        seq = lax.axis_index("seq")
        self.core = lax.rem(seq, 2)
        self.x = lax.div(seq, 2)
        self.y = lax.axis_index("data")
        self.dev = {
            "core": {"seq": seq + 1 - 2 * self.core},
            "x": {"seq": lax.rem(seq + 2, N_SEQ)},
            "y": {"data": 1 - self.y},
        }

    def greet(self):
        barrier = pltpu.get_barrier_semaphore()
        for dev in self.dev.values():
            pl.semaphore_signal(barrier, inc=1, device_id=dev, device_id_type=MESH)
        pl.semaphore_wait(barrier, 3)

    def copy(self, ends, axis):
        i = len(self.copies)

        def make():
            src, dst = ends()
            return pltpu.make_async_remote_copy(src_ref=src, dst_ref=dst, send_sem=self.send_sem.at[i], recv_sem=self.recv_sem.at[i],
                                                device_id=self.dev[axis], device_id_type=MESH)

        self.copies.append(make)
        return make


def rows_at(start, size):
    return pl.ds(pl.multiple_of(start, 16), size)


def sum_stages(links, acc, gat, stg, rcv, col0, n_col):
    half = acc.shape[0] // 2
    h0 = links.core * half
    every = pl.ds(col0, n_col)
    box = []
    for q in range(2):
        first, second = ("x", "y") if q == 0 else ("y", "x")
        k1, k2 = (links.x, links.y) if q == 0 else (links.y, links.x)
        box.append((q, first, second, k1, k2, pl.ds(col0 + q * (n_col // 2), n_col // 2)))
    n2, n4 = half // 2, half // 4

    def same(rows, cols):
        def ends():
            ref = gat.at[rows(), cols]
            return ref, ref
        return ends

    swap = links.copy(lambda: (stg[0], rcv[0]), "core")
    back = links.copy(same(lambda: rows_at(h0, half), every), "core")
    hops = [(
        links.copy(lambda q=q: (stg[1].at[q], rcv[1].at[q]), first),
        links.copy(lambda q=q: (stg[2].at[q], rcv[2].at[q]), second),
        links.copy(same(lambda k1=k1, k2=k2: rows_at(h0 + k1 * n2 + k2 * n4, n4), cols), second),
        links.copy(same(lambda k1=k1: rows_at(h0 + k1 * n2, n2), cols), first),
    ) for q, first, second, k1, k2, cols in box]

    def s1():
        stg[0][...] = acc[rows_at((1 - links.core) * half, half), every].astype(BF16)
        swap().start()

    def s2():
        swap().wait_recv()
        own = rows_at(h0, half)
        acc[own, every] = acc[own, every] + rcv[0][...].astype(F32)
        for q, first, second, k1, k2, cols in box:
            stg[1][q] = acc[rows_at(h0 + (1 - k1) * n2, n2), cols].astype(BF16)
            hops[q][0]().start()

    def s3():
        for q, first, second, k1, k2, cols in box:
            hops[q][0]().wait_recv()
            part = rows_at((1 - k2) * n4, n4)
            stg[2][q] = (acc[rows_at(h0 + k1 * n2 + (1 - k2) * n4, n4), cols] + rcv[1][q, part].astype(F32)).astype(BF16)
            hops[q][1]().start()

    def s4():
        for q, first, second, k1, k2, cols in box:
            hops[q][1]().wait_recv()
            part = rows_at(k2 * n4, n4)
            own = rows_at(h0 + k1 * n2 + k2 * n4, n4)
            gat[own, cols] = (acc[own, cols] + rcv[1][q, part].astype(F32) + rcv[2][q].astype(F32)).astype(BF16)
            hops[q][2]().start()

    def s5():
        for hop in hops:
            hop[2]().wait_recv()
            hop[3]().start()

    def s6():
        for hop in hops:
            hop[3]().wait_recv()
        back().start()

    def s7():
        back().wait_recv()

    return [s1, s2, s3, s4, s5, s6, s7]


def dc_stages(links, src, gat, stg, rcv):
    n_row = src.shape[0]
    half, quar, eigh = n_row // 2, n_row // 4, n_row // SUB
    h0 = links.core * half
    r0 = h0 + links.x * quar
    r_far = h0 + (1 - links.x) * quar
    y_own, y_far = links.y * n_row, (1 - links.y) * n_row

    def hop(start, size, axis):
        def ends():
            ref = gat.at[rows_at(start(), size), :]
            return ref, ref
        return links.copy(ends, axis)

    swap = links.copy(lambda: (stg[0], rcv[0]), "core")
    cross = links.copy(lambda: (stg[1], rcv[1]), "x")
    up_y = hop(lambda: y_own + r0, eigh, "y")
    down_x = hop(lambda: y_own + r0 + eigh, eigh, "x")
    up_x = hop(lambda: y_own + r0, eigh, "x")
    down_y = hop(lambda: y_own + r0 + eigh, eigh, "y")
    up_far = hop(lambda: y_far + r0, eigh, "x")
    down_far = hop(lambda: y_own + r_far + eigh, eigh, "y")
    back = [hop(lambda: y_own + h0, half, "core"), hop(lambda: y_far + h0, half, "core")]

    def s1():
        stg[0][...] = src[rows_at((1 - links.core) * half, half), :].astype(BF16)
        swap().start()

    def s2():
        swap().wait_recv()
        part = rows_at((1 - links.x) * quar, quar)
        stg[1][...] = (src[rows_at(r_far, quar), :] + rcv[0][part, :].astype(F32)).astype(BF16)
        cross().start()

    def s3():
        cross().wait_recv()
        part = rows_at(links.x * quar, quar)
        total = src[rows_at(r0, quar), :] + rcv[0][part, :].astype(F32) + rcv[1][...].astype(F32)
        gat[rows_at(y_own + r0, quar), :] = total.astype(BF16)
        for cp in (up_y, down_x, up_x, down_y):
            cp().start()

    def s4():
        up_y().wait_recv()
        up_far().start()
        down_x().wait_recv()
        down_far().start()

    def s5():
        for cp in (up_x, down_y, up_far, down_far):
            cp().wait_recv()
        for cp in back:
            cp().start()

    def s6():
        for cp in back:
            cp().wait_recv()

    return [s1, s2, s3, s4, s5, s6]


N_COPY = 10 * 4 + 1


def sum_scratch(n_row, n_col):
    half = n_row // 2
    return [pltpu.VMEM((half, n_col), BF16), pltpu.VMEM((2, half // 2, n_col // 2), BF16), pltpu.VMEM((2, half // 4, n_col // 2), BF16)]


W_CHUNK = 256


def backward_kernel(labels, pred, z_hbm, h_hbm, q0_ref, q1_ref, norm_ref, w_out, enc, da_out, g_enc_out, g_out_out, g_dc_out, far_out,
                    dz_all, h_all, da_all, da_part, dz0, dz1, dz2, dh0, dh1, dh2, w_out_t, z_ring, dw_enc, dw_out, dc_out, g_enc, g_out, g_dc,
                    es0, es1, es2, er0, er1, er2, ps0, ps1, ps2, pr0, pr1, pr2, qs0, qs1, qs2, qr0, qr1, qr2, ds0, ds1, dr0, dr1,
                    h_sem, z_sem, o_sem, send_sem, recv_sem):
    step = pl.program_id(0)
    lane = lax.broadcasted_iota(jnp.int32, (SUB, LANES), 1)
    sub = lax.broadcasted_iota(jnp.int32, (SUB, LANES), 0)
    n_j, n_v = w_out.shape
    utt_rows = UG * ROWS

    dzs, dhs = (dz0, dz1, dz2), (dh0, dh1, dh2)
    prev = jnp.maximum(step - 1, 0)
    z_slot = lax.rem(step, RING)

    def multiply(ug):
        dhs[ug][...] = dot(dzs[ug][...], w_out_t[...])[:, :n_j]

    def h_copy(utt):
        rows = pl.ds(pl.multiple_of(utt * utt_rows, 16), utt_rows)
        return pltpu.make_async_copy(h_hbm.at[rows, :], h_all.at[rows, :], h_sem.at[utt])

    def z_copy(utt):
        slot = lax.rem(utt, RING)
        return pltpu.make_async_copy(z_hbm.at[utt], z_ring.at[slot], z_sem.at[slot])

    links = Links(send_sem, recv_sem)
    far = links.copy(lambda: (pred, far_out), "y")
    e_st = sum_stages(links, dw_enc, g_enc, (es0, es1, es2), (er0, er1, er2), 0, n_v)
    p_st = sum_stages(links, dw_out, g_out, (ps0, ps1, ps2), (pr0, pr1, pr2), 0, n_v // 2)
    q_st = sum_stages(links, dw_out, g_out, (qs0, qs1, qs2), (qr0, qr1, qr2), n_v // 2, n_v // 2)
    c_st = dc_stages(links, dc_out, g_dc, (ds0, ds1), (dr0, dr1))

    @pl.when(step == 0)
    def _():
        links.greet()
        far().start()
        for utt in range(RING - 1):
            z_copy(utt).start()
            h_copy(utt).start()
        w_out_t[:, :n_j] = w_out[...].T
        w_out_t[:, n_j:] = jnp.zeros((n_v, w_out_t.shape[1] - n_j), BF16)

    def logit_grads(ug):
        shift = LANES - step
        lab_grp = label_column(labels, step, ug, sub)
        masks = [lab_grp - LANES * k == lane for k in range(n_v // LANES)]
        for t in range(0, T_LOC, 2):
            pair = []
            for idx in (ug * T_LOC + t, ug * T_LOC + t + 1):
                q0, q1, norm = [jnp.broadcast_to(pltpu.roll(ref[idx], shift, 1)[:, 0:1], (SUB, LANES)) for ref in (q0_ref, q1_ref, norm_ref)]
                row = (idx - ug * T_LOC) * SUB
                tiles = []
                for k in range(n_v // LANES):
                    z = z_ring[z_slot, ug, row:row + SUB, k * LANES:k * LANES + LANES]
                    g = jnp.exp2(z * LOG2E - norm) - jnp.where(masks[k], q1, 0.0)
                    tiles.append(g - jnp.where(lane == 0, q0, 0.0) if k == 0 else g)
                pair.append(jnp.concatenate(tiles, axis=1))
            rows = pl.ds(pl.multiple_of(step * utt_rows + ug * ROWS + t * SUB, 16), 16)
            dz = jnp.concatenate(pair, axis=0).astype(BF16)
            dz_all[rows, :] = dz
            dzs[ug][t * SUB:t * SUB + 16, :] = dz

    def hidden_grads(utt, ug):
        dc = None
        for t in range(0, T_LOC, 2):
            hid = h_all[pl.ds(pl.multiple_of(utt * utt_rows + ug * ROWS + t * SUB, 16), 16), :].astype(F32)
            ds = dhs[ug][t * SUB:t * SUB + 16, :] * (1.0 - hid * hid)
            both = ds[:SUB] + ds[SUB:]
            dc = both if dc is None else dc + both
            if ug > 0:
                ds = ds + da_part[t * SUB:t * SUB + 16, :]
            if ug < UG - 1:
                da_part[t * SUB:t * SUB + 16, :] = ds
            else:
                for k in range(2):
                    da_all[pl.ds(utt * T_LOC + t + k, 1), :] = jnp.sum(ds[SUB * k:SUB * k + SUB], axis=0, keepdims=True)
        dc_out[pl.ds(pl.multiple_of(utt * N_UP + ug * SUB, SUB), SUB), :] = dc

    @pl.when(step + RING - 1 < N_UTT)
    def _():
        z_copy(step + RING - 1).start()
        h_copy(step + RING - 1).start()

    @pl.when(step < N_UTT)
    def _():
        h_copy(step).wait()
        z_copy(step).wait()
        multiply(2)
        logit_grads(0)
        hidden_grads(prev, 1)
        multiply(0)
        logit_grads(1)
        hidden_grads(prev, 2)
        multiply(1)
        logit_grads(2)
        hidden_grads(step, 0)

    @pl.when(step == N_UTT)
    def _():
        multiply(2)
        hidden_grads(prev, 1)
        hidden_grads(prev, 2)
        da = da_all[...].astype(BF16)
        da_out[...] = da
        dw_enc[...] = dot(da, enc[...], ((0,), (0,)))
        e_st[0]()
        c_st[0]()

    plan = [
        ((e_st[1], c_st[1]), ()),
        ((), (p_st[0],)),
        ((e_st[2], c_st[2], p_st[1]), ()),
        ((e_st[3], c_st[3], p_st[2]), (q_st[0], e_st[4], p_st[3], c_st[4], q_st[1], e_st[5], p_st[4], q_st[2], c_st[5], q_st[3], p_st[5], e_st[6], q_st[4])),
    ]
    for part, (lo, hi) in enumerate(((0, 3 * LANES), (3 * LANES, n_j))):
        @pl.when(step > N_UTT)
        def _(lo=lo, hi=hi):
            cols = pl.ds(pl.multiple_of((step - N_UTT - 1) * W_CHUNK, W_CHUNK), W_CHUNK)
            dw_out[lo:hi, cols] = dot(h_all[:, lo:hi], dz_all[:, cols], ((0,), (0,)))

        for n, stages in enumerate(plan):
            if stages[part]:
                @pl.when(step == N_UTT + 1 + n)
                def _(stages=stages[part]):
                    for stage in stages:
                        stage()

    @pl.when(step == N_UTT + len(plan))
    def _():
        out_dc = pltpu.make_async_copy(g_dc, g_dc_out, o_sem.at[0])
        out_dc.start()
        out_enc = pltpu.make_async_copy(g_enc, g_enc_out, o_sem.at[1])
        out_enc.start()
        p_st[6]()
        q_st[5]()
        q_st[6]()
        out_out = pltpu.make_async_copy(g_out, g_out_out, o_sem.at[2])
        out_out.start()
        far().wait_recv()
        for cp in links.copies:
            cp().wait_send()
        out_dc.wait()
        out_enc.wait()
        out_out.wait()


def joint_backward(labels, pred, z, h, q0, q1, norm, w_out, enc):
    n_j, n_v = w_out.shape
    n_cell = N_UTT * UG * ROWS
    n_dc = N_UTT * N_UP
    full = lambda shape: pl.BlockSpec(shape, lambda i: (0,) * len(shape), pipeline_mode=pl.Buffered(1))
    return pl.pallas_call(
        backward_kernel,
        grid=(N_UTT + 1 + n_v // W_CHUNK,),
        in_specs=[
            pl.BlockSpec(memory_space=pltpu.SMEM),
            *[pl.BlockSpec(memory_space=pl.ANY)] * 3,
            full(q0.shape), full(q1.shape), full(norm.shape), full(w_out.shape), full(enc.shape),
        ],
        out_specs=[full((N_UTT * T_LOC, n_j))] + [pl.BlockSpec(memory_space=pl.ANY)] * 4,
        out_shape=[
            jax.ShapeDtypeStruct((N_UTT * T_LOC, n_j), BF16),
            jax.ShapeDtypeStruct((n_j, n_v), BF16),
            jax.ShapeDtypeStruct((n_j, n_v), BF16),
            jax.ShapeDtypeStruct((2 * n_dc, n_j), BF16),
            jax.ShapeDtypeStruct(pred.shape, BF16),
        ],
        scratch_shapes=[
            pltpu.VMEM((n_cell, n_v), BF16), pltpu.VMEM((n_cell, n_j), BF16), pltpu.VMEM((N_UTT * T_LOC, n_j), F32),
            pltpu.VMEM((ROWS, n_j), F32),
            *[pltpu.VMEM((ROWS, n_v), BF16)] * 3, *[pltpu.VMEM((ROWS, n_j), F32)] * 3,
            pltpu.VMEM((n_v, n_j + (-n_j) % 256), BF16), pltpu.VMEM((RING, UG, ROWS, n_v), F32),
            pltpu.VMEM((n_j, n_v), F32), pltpu.VMEM((n_j, n_v), F32), pltpu.VMEM((n_dc, n_j), F32),
            pltpu.VMEM((n_j, n_v), BF16), pltpu.VMEM((n_j, n_v), BF16), pltpu.VMEM((2 * n_dc, n_j), BF16),
            *sum_scratch(n_j, n_v) * 2, *sum_scratch(n_j, n_v // 2) * 4,
            *[pltpu.VMEM((n_dc // 2, n_j), BF16), pltpu.VMEM((n_dc // 4, n_j), BF16)] * 2,
            pltpu.SemaphoreType.DMA((N_UTT,)), pltpu.SemaphoreType.DMA((RING,)), pltpu.SemaphoreType.DMA((3,)),
            pltpu.SemaphoreType.DMA((N_COPY,)), pltpu.SemaphoreType.DMA((N_COPY,)),
        ],
        compiler_params=pltpu.CompilerParams(collective_id=1, has_side_effects=True, vmem_limit_bytes=VMEM_FULL),
        name="joint_backward",
    )(labels, pred, z, h.reshape(n_cell, n_j), q0, q1, norm, w_out, enc)


def finish_kernel(loss, g_enc, g_out, g_dc, pred, pred_far, w_pred, da, w_enc, o_loss, o_enc, o_pred, o_wenc, o_wpred, o_wout,
                  v_enc, v_pred, v_wenc, v_wpred, v_wout, sem):
    y = lax.axis_index("data")
    o_loss[...] = loss[0:1, :N_UTT]
    jobs = []

    def put(src, dst, i):
        cp = pltpu.make_async_copy(src, dst, sem.at[i])
        cp.start()
        jobs.append(cp)

    v_wenc[...] = g_enc[...].astype(F32).T
    put(v_wenc, o_wenc, 0)
    v_wout[...] = g_out[...].astype(F32)
    put(v_wout, o_wout, 1)
    n_r = pred.shape[0]
    dc_own, dc_far = g_dc[rows_at(y * n_r, n_r), :], g_dc[rows_at((1 - y) * n_r, n_r), :]
    v_wpred[...] = dot(pred[...], dc_own, ((0,), (0,))) + dot(pred_far[...], dc_far, ((0,), (0,)))
    put(v_wpred, o_wpred, 2)
    v_pred[...] = dot(dc_own, w_pred[...], ((1,), (1,)))
    put(v_pred, o_pred, 3)
    v_enc[...] = dot(da[...], w_enc[...], ((1,), (1,))).astype(BF16)
    put(v_enc, o_enc, 4)
    for cp in jobs:
        cp.wait()


def finish(loss, g_enc, g_out, g_dc, pred, pred_far, w_pred, da, w_enc):
    vm = pl.BlockSpec(memory_space=pltpu.VMEM)
    outs = [(pred.shape, BF16), (pred.shape, F32), (w_pred.shape, F32), (w_pred.shape, F32), (w_pred.shape[::-1], F32)]
    return pl.pallas_call(
        finish_kernel,
        in_specs=[vm] * 9,
        out_specs=[vm] + [pl.BlockSpec(memory_space=pl.ANY)] * 5,
        out_shape=[jax.ShapeDtypeStruct((1, N_UTT), F32)] + [jax.ShapeDtypeStruct(*o) for o in outs],
        scratch_shapes=[pltpu.VMEM(*o) for o in outs] + [pltpu.SemaphoreType.DMA((5,))],
        compiler_params=pltpu.CompilerParams(vmem_limit_bytes=VMEM_FULL),
        name="finish",
    )(loss, g_enc, g_out, g_dc, pred, pred_far, w_pred, da, w_enc)


def solution(mesh):
    utt_rows = P(("part", "data"))
    utt_mats = P(("part", "data"), None)
    utt_cube = P(("part", "data"), None, None)
    enc_spec = P(("part", "data"), "seq", None)
    weight_in = P(None, None)
    weight_out = P("part", None)

    def body(enc_loc, pred_loc, w_enc, w_pred, w_out, labels, frame_len, label_len):
        n_h = enc_loc.shape[2]
        enc2 = enc_loc.reshape(N_UTT * T_LOC, n_h)
        pred2 = pred_loc.reshape(N_UTT * N_UP, n_h)
        z, h, stat, norm = joint_forward(labels, enc2, pred2, w_enc, w_pred, w_out)
        q0, q1, norm, loss = lattice(stat, norm, frame_len, label_len)
        da, g_enc, g_out, g_dc, pred_far = joint_backward(labels, pred2, z, h, q0, q1, norm, w_out, enc2)
        loss, grad_enc, grad_pred, grad_w_enc, grad_w_pred, grad_w_out = finish(loss, g_enc, g_out, g_dc, pred2, pred_far, w_pred, da, w_enc)
        return loss.reshape(N_UTT), grad_enc.reshape(enc_loc.shape), grad_pred.reshape(pred_loc.shape), grad_w_enc, grad_w_pred, grad_w_out

    return jax.shard_map(body, mesh=mesh, in_specs=(enc_spec, utt_cube, weight_in, weight_in, weight_in, utt_mats, utt_rows, utt_rows), out_specs=(utt_rows, enc_spec, utt_cube, weight_out, weight_out, weight_out), check_vma=False)
```

time: 281 us -> 124 us (0.44)
  waiting for transfers between devices: 116 us -> 0 us
  Pallas kernels: 81.8 us -> 123 us
  blocking collectives: 40.7 us -> 0 us
  local copies, waits for them, and re-layouts: 17.1 us -> 0 us
  between operations: 14.1 us -> 0.82 us
  matrix products: 10.7 us -> 0 us
    psum x2 -> x0, waiting for transfers between devices: 116 us -> none  [the longest x1 67.7 us: body(): grad_w_pred = lax.psum(grad_w_pred, 'data')]
    pallas_call x3 -> x4, Pallas kernels: 81.8 us -> 123 us  [the longest x1 72.1 us: joint_backward(): pl.pallas_call(backward_kernel, grid=(N_UTT + 1 + n_v // W_CHUNK,), in_sp...]
    psum x1 -> x0, blocking collectives: 40.7 us -> none  [body(): dc = lax.psum(dc, 'seq').astype(BF16).reshape(N_UTT * N_UP, -1)]
    unnamed x14 -> x0, local copies, waits for them, and re-layouts: 11.5 us -> none
    dot_general x4 -> x0, matrix products: 10.7 us -> none  [dot(): lax.dot_general(lhs, rhs, (dims, ((), ())), preferred_element_type=F32)]
  transfers between devices with their start and end apart: 2 -> 0, of which waited for: 2 -> 0; matrix products, arithmetic and copies ran while one was open for 4% -> 0% of each run, Pallas kernels for 0% -> 0%
where the time goes in v3:
time: 124 us
  Pallas kernels  123 us (99%)
    pallas_call x1, Pallas kernels, joint_backward(): pl.pallas_call(backward_kernel, grid=(N_UTT + 1 + n_v // W_CHUNK,), in_sp...  72.1 us
    pallas_call x1, Pallas kernels, joint_forward(): pl.pallas_call(forward_kernel, grid=(N_UTT,), in_specs=[pl.BlockSpec(memo...  28.4 us
    pallas_call x1, Pallas kernels, lattice(): pl.pallas_call(lattice_kernel, in_specs=[vm] * 2 + [pl.BlockSpec(memory_s...  11.5 us
    pallas_call x1, Pallas kernels, finish(): pl.pallas_call(finish_kernel, in_specs=[vm] * 9, out_specs=[vm] + [pl.Blo...  10.8 us

profile of v3, /device:TPU:0, one launch (start us, length us, event | category | flops | bytes accessed | tf_op | source)
XLA Modules:
  0.0 123.7 jit_solution(3301597660345563044)
XLA Ops:
  0.6 28.4 %joint_forward.1 = (f32[16,3,192,1024]{3,2,1,0:T(8,128)}, bf16[16,3,192,640]{3,2,1,0:T(8,128)(2,1)}, f32[18,8,128]{2,1,0:T(8,128)}, f32[72,8,128]{2,1,0:T(8,128)}) custom-call(s32[16,23]{1,0:T(8,128)} %labels.3, bf16[384,1024]{1,0:T(8,128)(2,1)} %bitcast.10, bf16[384,1024]{1,0:T(8,128)(2,1)} %bitcast.7, bf16[1024,640]{1,0:T(8,128)(2,1)} %w_enc.3, ...), custom_call_target="tpu_custom_call" | custom-call | tf_op jit(solution)/shard_map/joint_forward/pallas_call | solution.py:126
  29.1 11.5 %lattice.1 = (f32[72,8,128]{2,1,0:T(8,128)}, f32[72,8,128]{2,1,0:T(8,128)}, f32[72,8,128]{2,1,0:T(8,128)}, f32[8,128]{1,0:T(8,128)}) custom-call(f32[18,8,128]{2,1,0:T(8,128)} %get-tuple-element.25.stat, f32[72,8,128]{2,1,0:T(8,128)} %get-tuple-element.26.norm, s32[16]{0:T(128)} %flen.1, s32[16]{0:T(128)} %llen.1), custom_call_target="tpu_custom_call" | custom-call | tf_op jit(solution)/shard_map/lattice/pallas_call | solution.py:253
  40.6 72.1 %joint_backward.1 = (bf16[384,640]{1,0:T(8,128)(2,1)}, bf16[640,1024]{1,0:T(8,128)(2,1)}, bf16[640,1024]{1,0:T(8,128)(2,1)}, bf16[768,640]{1,0:T(8,128)(2,1)}, bf16[384,1024]{1,0:T(8,128)(2,1)}) custom-call(s32[16,23]{1,0:T(8,128)} %labels.3, bf16[384,1024]{1,0:T(8,128)(2,1)} %bitcast.8, f32[16,3,192,1024]{3,2,1,0:T(8,128)} %get-tuple-element.28.z_hbm, ...), custom_call_target="tpu_custom_call" | custom-call | tf_op jit(solution)/shard_map/joint_backward/pallas_call | solution.py:592
  112.8 10.8 %finish.1 = (f32[1,16]{1,0:T(1,128)}, bf16[384,1024]{1,0:T(8,128)(2,1)}, f32[384,1024]{1,0:T(8,128)}, f32[1024,640]{1,0:T(8,128)}, f32[1024,640]{1,0:T(8,128)}, /*index=5*/f32[640,1024]{1,0:T(8,128)}) custom-call(f32[8,128]{1,0:T(8,128)} %get-tuple-element.27.loss, bf16[640,1024]{1,0:T(8,128)(2,1)} %get-tuple-element.33.g_enc, ...), custom_call_target="tpu_custom_call" | custom-call | tf_op jit(solution)/shard_map/finish/pallas_call | solution.py:655

commit v4 on v3

--- a/solution.py
+++ b/solution.py
@@ -34,12 +34,11 @@
 def label_column(labels, utt, ug, sub):
     col = jnp.zeros((SUB, LANES), jnp.int32)
     for k in range(SUB):
-        if ug * SUB + k < N_UP - 1:
-            col = jnp.where(sub == k, labels[utt, ug * SUB + k], col)
+        col = jnp.where(sub == k, labels[utt, jnp.minimum(ug * SUB + k, N_UP - 2)], col)
     return col
 
 
-def forward_kernel(labels, enc, pred, w_enc, w_pred, w_out, z_hbm, h_hbm, stat_out, norm_out, act_e, act_p, h_next, z_last, z_ring, h_ring, z_sem, h_sem):
+def forward_kernel(labels, llen, enc, pred, w_enc, w_pred, w_out, z_hbm, h_hbm, stat_out, norm_out, act_e, act_p, h_next, z_last, z_ring, h_ring, z_sem, h_sem):
     step = pl.program_id(0)
     lane = lax.broadcasted_iota(jnp.int32, (SUB, LANES), 1)
     sub = lax.broadcasted_iota(jnp.int32, (SUB, LANES), 0)
@@ -96,37 +95,52 @@
             cp.wait()
 
     slot = lax.rem(step, RING)
-    z_out, h_out = z_ring.at[pl.ds(slot, 1)], h_ring.at[pl.ds(slot, 1)]
-    h_out[0, 0] = h_next[...]
-    z_out[0, 0] = dot(h_next[...], w_out[...])
-    hidden(step, 1, h_out.at[0, 1])
-    soften(step - 1, 2, z_last)
-    z_out[0, 1] = dot(h_out[0, 1], w_out[...])
-    hidden(step, 2, h_out.at[0, 2])
-    soften(step, 0, z_out.at[0, 0])
-    z_two = dot(h_out[0, 2], w_out[...])
-    z_last[...] = z_two
-    z_out[0, 2] = z_two
-    hidden(jnp.minimum(step + 1, N_UTT - 1), 0, h_next)
-    soften(step, 1, z_out.at[0, 1])
+    z_out, h_out = z_ring.at[slot], h_ring.at[slot]
+    groups = lax.div(llen[step], SUB) + 1
+    last_of = lambda utt: lax.div(llen[utt], SUB)
+
+    def utterance(n_grp):
+        h_out[0] = h_next[...]
+        for ug in range(n_grp):
+            z = dot(h_out[ug] if ug else h_next[...], w_out[...])
+            z_out[ug] = z
+            if ug == 0:
+                soften(step - 1, last_of(jnp.maximum(step - 1, 0)), z_last)
+            else:
+                soften(step, ug - 1, z_out.at[ug - 1])
+            if ug < n_grp - 1:
+                hidden(step, ug + 1, h_out.at[ug + 1])
+            else:
+                z_last[...] = z
+                hidden(jnp.minimum(step + 1, N_UTT - 1), 0, h_next)
+
+        if n_grp < UG:
+            @pl.when(step < RING)
+            def _():
+                for ug in range(n_grp, UG):
+                    z_out[ug] = jnp.zeros(z_out.shape[1:], F32)
+                    h_out[ug] = jnp.zeros(h_out.shape[1:], BF16)
+
+    for n_grp in range(1, UG + 1):
+        pl.when(groups == n_grp)(functools.partial(utterance, n_grp))
     for cp in puts(step):
         cp.start()
 
     @pl.when(step == N_UTT - 1)
     def _():
-        soften(step, 2, z_last)
+        soften(step, last_of(step), z_last)
         for back in range(RING - 1, -1, -1):
             for cp in puts(step - back):
                 cp.wait()
 
 
-def joint_forward(labels, enc, pred, w_enc, w_pred, w_out):
+def joint_forward(labels, llen, enc, pred, w_enc, w_pred, w_out):
     n_j, n_v = w_out.shape
     full = lambda shape: pl.BlockSpec(shape, lambda i: (0,) * len(shape), pipeline_mode=pl.Buffered(1))
     return pl.pallas_call(
         forward_kernel,
         grid=(N_UTT,),
-        in_specs=[pl.BlockSpec(memory_space=pltpu.SMEM)] + [full(v.shape) for v in (enc, pred, w_enc, w_pred, w_out)],
+        in_specs=[pl.BlockSpec(memory_space=pltpu.SMEM)] * 2 + [full(v.shape) for v in (enc, pred, w_enc, w_pred, w_out)],
         out_specs=[
             pl.BlockSpec(memory_space=pl.ANY),
             pl.BlockSpec(memory_space=pl.ANY),
@@ -144,7 +158,7 @@
             pltpu.SemaphoreType.DMA((RING,)), pltpu.SemaphoreType.DMA((RING,))],
         compiler_params=pltpu.CompilerParams(vmem_limit_bytes=VMEM_FULL),
         name="joint_forward",
-    )(labels, enc, pred, w_enc, w_pred, w_out)
+    )(labels, llen, enc, pred, w_enc, w_pred, w_out)
 
 
 def lae2(x, y):
@@ -427,7 +441,7 @@
     return [s1, s2, s3, s4, s5, s6]
 
 
-N_COPY = 10 * 4 + 1
+N_COPY = 10 * 5 + 1
 
 
 def sum_scratch(n_row, n_col):
@@ -440,7 +454,7 @@
 
 def backward_kernel(labels, pred, z_hbm, h_hbm, q0_ref, q1_ref, norm_ref, w_out, enc, da_out, g_enc_out, g_out_out, g_dc_out, far_out,
                     dz_all, h_all, da_all, da_part, dz0, dz1, dz2, dh0, dh1, dh2, w_out_t, z_ring, dw_enc, dw_out, dc_out, g_enc, g_out, g_dc,
-                    es0, es1, es2, er0, er1, er2, ps0, ps1, ps2, pr0, pr1, pr2, qs0, qs1, qs2, qr0, qr1, qr2, ds0, ds1, dr0, dr1,
+                    es0, es1, es2, er0, er1, er2, ps0, ps1, ps2, pr0, pr1, pr2, qs0, qs1, qs2, qr0, qr1, qr2, rs0, rs1, rs2, rr0, rr1, rr2, ds0, ds1, dr0, dr1,
                     h_sem, z_sem, o_sem, send_sem, recv_sem):
     step = pl.program_id(0)
     lane = lax.broadcasted_iota(jnp.int32, (SUB, LANES), 1)
@@ -467,7 +481,8 @@
     far = links.copy(lambda: (pred, far_out), "y")
     e_st = sum_stages(links, dw_enc, g_enc, (es0, es1, es2), (er0, er1, er2), 0, n_v)
     p_st = sum_stages(links, dw_out, g_out, (ps0, ps1, ps2), (pr0, pr1, pr2), 0, n_v // 2)
-    q_st = sum_stages(links, dw_out, g_out, (qs0, qs1, qs2), (qr0, qr1, qr2), n_v // 2, n_v // 2)
+    q_st = sum_stages(links, dw_out, g_out, (qs0, qs1, qs2), (qr0, qr1, qr2), n_v // 2, n_v // 4)
+    r_st = sum_stages(links, dw_out, g_out, (rs0, rs1, rs2), (rr0, rr1, rr2), n_v // 2 + n_v // 4, n_v // 4)
     c_st = dc_stages(links, dc_out, g_dc, (ds0, ds1), (dr0, dr1))
 
     @pl.when(step == 0)
@@ -547,10 +562,12 @@
         c_st[0]()
 
     plan = [
-        ((e_st[1], c_st[1]), ()),
-        ((), (p_st[0],)),
-        ((e_st[2], c_st[2], p_st[1]), ()),
-        ((e_st[3], c_st[3], p_st[2]), (q_st[0], e_st[4], p_st[3], c_st[4], q_st[1], e_st[5], p_st[4], q_st[2], c_st[5], q_st[3], p_st[5], e_st[6], q_st[4])),
+        ((c_st[1], e_st[1]), ()),
+        ((), (c_st[2], p_st[0])),
+        ((e_st[2], p_st[1]), ()),
+        ((e_st[3], q_st[0]), (
+            r_st[0], p_st[2], q_st[1], r_st[1], c_st[3], p_st[3], r_st[2], q_st[2], e_st[4], c_st[4], q_st[3], r_st[3], p_st[4],
+            q_st[4], r_st[4], p_st[5], e_st[5], q_st[5])),
     ]
     for part, (lo, hi) in enumerate(((0, 3 * LANES), (3 * LANES, n_j))):
         @pl.when(step > N_UTT)
@@ -567,15 +584,18 @@
 
     @pl.when(step == N_UTT + len(plan))
     def _():
-        out_dc = pltpu.make_async_copy(g_dc, g_dc_out, o_sem.at[0])
-        out_dc.start()
+        p_st[6]()
+        r_st[5]()
+        r_st[6]()
+        e_st[6]()
         out_enc = pltpu.make_async_copy(g_enc, g_enc_out, o_sem.at[1])
         out_enc.start()
-        p_st[6]()
-        q_st[5]()
         q_st[6]()
         out_out = pltpu.make_async_copy(g_out, g_out_out, o_sem.at[2])
         out_out.start()
+        c_st[5]()
+        out_dc = pltpu.make_async_copy(g_dc, g_dc_out, o_sem.at[0])
+        out_dc.start()
         far().wait_recv()
         for cp in links.copies:
             cp().wait_send()
@@ -612,7 +632,7 @@
             pltpu.VMEM((n_v, n_j + (-n_j) % 256), BF16), pltpu.VMEM((RING, UG, ROWS, n_v), F32),
             pltpu.VMEM((n_j, n_v), F32), pltpu.VMEM((n_j, n_v), F32), pltpu.VMEM((n_dc, n_j), F32),
             pltpu.VMEM((n_j, n_v), BF16), pltpu.VMEM((n_j, n_v), BF16), pltpu.VMEM((2 * n_dc, n_j), BF16),
-            *sum_scratch(n_j, n_v) * 2, *sum_scratch(n_j, n_v // 2) * 4,
+            *sum_scratch(n_j, n_v) * 2, *sum_scratch(n_j, n_v // 2) * 2, *sum_scratch(n_j, n_v // 4) * 4,
             *[pltpu.VMEM((n_dc // 2, n_j), BF16), pltpu.VMEM((n_dc // 4, n_j), BF16)] * 2,
             pltpu.SemaphoreType.DMA((N_UTT,)), pltpu.SemaphoreType.DMA((RING,)), pltpu.SemaphoreType.DMA((3,)),
             pltpu.SemaphoreType.DMA((N_COPY,)), pltpu.SemaphoreType.DMA((N_COPY,)),
@@ -622,45 +642,62 @@
     )(labels, pred, z, h.reshape(n_cell, n_j), q0, q1, norm, w_out, enc)
 
 
-def finish_kernel(loss, g_enc, g_out, g_dc, pred, pred_far, w_pred, da, w_enc, o_loss, o_enc, o_pred, o_wenc, o_wpred, o_wout,
-                  v_enc, v_pred, v_wenc, v_wpred, v_wout, sem):
+def finish_kernel(loss, *refs):
+    ins, o_loss, outs = refs[:FIN_IN], refs[FIN_IN], refs[FIN_IN + 1:FIN_IN + 1 + FIN_OUT]
+    bufs, vals, in_sem, out_sem = refs[FIN_IN + 1 + FIN_OUT:-FIN_OUT - 2], refs[-FIN_OUT - 2:-2], refs[-2], refs[-1]
+    g_out, g_enc, da, w_enc, g_dc, w_pred, pred, pred_far = bufs
+    v_wout, v_wenc, v_enc, v_pred, v_wpred = vals
+    loads = [pltpu.make_async_copy(src, dst, in_sem.at[k]) for k, (src, dst) in enumerate(zip(ins, bufs))]
+    stores = [pltpu.make_async_copy(src, dst, out_sem.at[k]) for k, (src, dst) in enumerate(zip(vals, outs))]
+    for cp in loads:
+        cp.start()
     y = lax.axis_index("data")
+    n_r = pred.shape[0]
     o_loss[...] = loss[0:1, :N_UTT]
-    jobs = []
-
-    def put(src, dst, i):
-        cp = pltpu.make_async_copy(src, dst, sem.at[i])
-        cp.start()
-        jobs.append(cp)
-
+    loads[0].wait()
+    v_wout[...] = g_out[...].astype(F32)
+    stores[0].start()
+    loads[1].wait()
     v_wenc[...] = g_enc[...].astype(F32).T
-    put(v_wenc, o_wenc, 0)
-    v_wout[...] = g_out[...].astype(F32)
-    put(v_wout, o_wout, 1)
-    n_r = pred.shape[0]
-    dc_own, dc_far = g_dc[rows_at(y * n_r, n_r), :], g_dc[rows_at((1 - y) * n_r, n_r), :]
+    stores[1].start()
+    loads[2].wait()
+    loads[3].wait()
+    v_enc[...] = dot(da[...], w_enc[...], ((1,), (1,))).astype(BF16)
+    stores[2].start()
+    loads[4].wait()
+    loads[5].wait()
+    dc_own = g_dc[rows_at(y * n_r, n_r), :]
+    dc_far = g_dc[rows_at((1 - y) * n_r, n_r), :]
+    v_pred[...] = dot(dc_own, w_pred[...], ((1,), (1,)))
+    stores[3].start()
+    loads[6].wait()
+    loads[7].wait()
     v_wpred[...] = dot(pred[...], dc_own, ((0,), (0,))) + dot(pred_far[...], dc_far, ((0,), (0,)))
-    put(v_wpred, o_wpred, 2)
-    v_pred[...] = dot(dc_own, w_pred[...], ((1,), (1,)))
-    put(v_pred, o_pred, 3)
-    v_enc[...] = dot(da[...], w_enc[...], ((1,), (1,))).astype(BF16)
-    put(v_enc, o_enc, 4)
-    for cp in jobs:
+    stores[4].start()
+    for cp in stores:
         cp.wait()
+
+
+FIN_IN = 8
+FIN_OUT = 5
 
 
 def finish(loss, g_enc, g_out, g_dc, pred, pred_far, w_pred, da, w_enc):
     vm = pl.BlockSpec(memory_space=pltpu.VMEM)
-    outs = [(pred.shape, BF16), (pred.shape, F32), (w_pred.shape, F32), (w_pred.shape, F32), (w_pred.shape[::-1], F32)]
-    return pl.pallas_call(
+    hbm = pl.BlockSpec(memory_space=pl.ANY)
+    ins = (g_out, g_enc, da, w_enc, g_dc, w_pred, pred, pred_far)
+    outs = [(g_out.shape, F32), (w_enc.shape, F32), (pred.shape, BF16), (pred.shape, F32), (w_pred.shape, F32)]
+    loss, grad_w_out, grad_w_enc, grad_enc, grad_pred, grad_w_pred = pl.pallas_call(
         finish_kernel,
-        in_specs=[vm] * 9,
-        out_specs=[vm] + [pl.BlockSpec(memory_space=pl.ANY)] * 5,
+        in_specs=[vm] + [hbm] * FIN_IN,
+        out_specs=[vm] + [hbm] * FIN_OUT,
         out_shape=[jax.ShapeDtypeStruct((1, N_UTT), F32)] + [jax.ShapeDtypeStruct(*o) for o in outs],
-        scratch_shapes=[pltpu.VMEM(*o) for o in outs] + [pltpu.SemaphoreType.DMA((5,))],
+        scratch_shapes=[pltpu.VMEM(v.shape, v.dtype) for v in ins] + [pltpu.VMEM(*o) for o in outs]
+        + [pltpu.SemaphoreType.DMA((FIN_IN,)), pltpu.SemaphoreType.DMA((FIN_OUT,))],
         compiler_params=pltpu.CompilerParams(vmem_limit_bytes=VMEM_FULL),
         name="finish",
-    )(loss, g_enc, g_out, g_dc, pred, pred_far, w_pred, da, w_enc)
+    )(loss, *ins)
+    return loss, grad_enc, grad_pred, grad_w_enc, grad_w_pred, grad_w_out
 
 
 def solution(mesh):
@@ -675,7 +712,7 @@
         n_h = enc_loc.shape[2]
         enc2 = enc_loc.reshape(N_UTT * T_LOC, n_h)
         pred2 = pred_loc.reshape(N_UTT * N_UP, n_h)
-        z, h, stat, norm = joint_forward(labels, enc2, pred2, w_enc, w_pred, w_out)
+        z, h, stat, norm = joint_forward(labels, label_len, enc2, pred2, w_enc, w_pred, w_out)
         q0, q1, norm, loss = lattice(stat, norm, frame_len, label_len)
         da, g_enc, g_out, g_dc, pred_far = joint_backward(labels, pred2, z, h, q0, q1, norm, w_out, enc2)
         loss, grad_enc, grad_pred, grad_w_enc, grad_w_pred, grad_w_out = finish(loss, g_enc, g_out, g_dc, pred2, pred_far, w_pred, da, w_enc)

time: 124 us -> 116 us (0.935)
  Pallas kernels: 123 us -> 116 us
    pallas_call x1, Pallas kernels: 28.4 us -> 25 us  [joint_forward(): pl.pallas_call(forward_kernel, grid=(N_UTT,), in_specs=[pl.BlockSpec(memo...]
    pallas_call x1, Pallas kernels: 72.1 us -> 69.5 us  [joint_backward(): pl.pallas_call(backward_kernel, grid=(N_UTT + 1 + n_v // W_CHUNK,), in_sp...]
where the time goes in v4:
time: 116 us; the launch traced here: 117 us
  Pallas kernels  116 us (100%)
    pallas_call x1, Pallas kernels, joint_backward(): pl.pallas_call(backward_kernel, grid=(N_UTT + 1 + n_v // W_CHUNK,), in_sp...  69.5 us
    pallas_call x1, Pallas kernels, joint_forward(): pl.pallas_call(forward_kernel, grid=(N_UTT,), in_specs=[pl.BlockSpec(memo...  25 us
    pallas_call x1, Pallas kernels, lattice(): pl.pallas_call(lattice_kernel, in_specs=[vm] * 2 + [pl.BlockSpec(memory_s...  11.5 us
    pallas_call x1, Pallas kernels, finish(): pl.pallas_call(finish_kernel, in_specs=[vm] + [hbm] * FIN_IN, out_specs=[...  9.99 us

profile of v4, /device:TPU:0, one launch (start us, length us, event | category | flops | bytes accessed | tf_op | source)
XLA Modules:
  0.0 116.8 jit_solution(2417689726983918920)
XLA Ops:
  0.6 25.0 %joint_forward.1 = (f32[16,3,192,1024]{3,2,1,0:T(8,128)}, bf16[16,3,192,640]{3,2,1,0:T(8,128)(2,1)}, f32[18,8,128]{2,1,0:T(8,128)}, f32[72,8,128]{2,1,0:T(8,128)}) custom-call(s32[16,23]{1,0:T(8,128)} %labels.3, s32[16]{0:T(128)} %llen.3, bf16[384,1024]{1,0:T(8,128)(2,1)} %bitcast.10, bf16[384,1024]{1,0:T(8,128)(2,1)} %bitcast.7, bf16[1024,640]{1,0:T(8,128)(2,1)} %refs_3_.1, ...), custom_call_target="tpu_custom_call" | custom-call | tf_op jit(solution)/shard_map/joint_forward/pallas_call | solution.py:140
  25.6 11.5 %lattice.1 = (f32[72,8,128]{2,1,0:T(8,128)}, f32[72,8,128]{2,1,0:T(8,128)}, f32[72,8,128]{2,1,0:T(8,128)}, f32[8,128]{1,0:T(8,128)}) custom-call(f32[18,8,128]{2,1,0:T(8,128)} %get-tuple-element.25.stat, f32[72,8,128]{2,1,0:T(8,128)} %get-tuple-element.26.norm, s32[16]{0:T(128)} %flen.1, s32[16]{0:T(128)} %llen.3), custom_call_target="tpu_custom_call" | custom-call | tf_op jit(solution)/shard_map/lattice/pallas_call | solution.py:267
  37.2 69.5 %joint_backward.1 = (bf16[384,640]{1,0:T(8,128)(2,1)}, bf16[640,1024]{1,0:T(8,128)(2,1)}, bf16[640,1024]{1,0:T(8,128)(2,1)}, bf16[768,640]{1,0:T(8,128)(2,1)}, bf16[384,1024]{1,0:T(8,128)(2,1)}) custom-call(s32[16,23]{1,0:T(8,128)} %labels.3, bf16[384,1024]{1,0:T(8,128)(2,1)} %bitcast.8, f32[16,3,192,1024]{3,2,1,0:T(8,128)} %get-tuple-element.28.z_hbm, ...), custom_call_target="tpu_custom_call" | custom-call | tf_op jit(solution)/shard_map/joint_backward/pallas_call | solution.py:612
  106.7 10.0 %finish.1 = (f32[1,16]{1,0:T(1,128)}, f32[640,1024]{1,0:T(8,128)}, f32[1024,640]{1,0:T(8,128)}, bf16[384,1024]{1,0:T(8,128)(2,1)}, f32[384,1024]{1,0:T(8,128)}, /*index=5*/f32[1024,640]{1,0:T(8,128)}) custom-call(f32[8,128]{1,0:T(8,128)} %get-tuple-element.27.loss, bf16[640,1024]{1,0:T(8,128)(2,1)} %get-tuple-element.33.refs_0_, ...), custom_call_target="tpu_custom_call" | custom-call | tf_op jit(solution)/shard_map/finish/pallas_call | solution.py:690

commit v5 on v4

--- a/solution.py
+++ b/solution.py
@@ -68,13 +68,13 @@
                 t = t4 * 4 + k
                 z = [src[t * SUB:t * SUB + SUB, c * LANES:c * LANES + LANES] for c in range(n_v // LANES)]
                 top = functools.reduce(jnp.maximum, z)
-                tot = functools.reduce(jnp.add, [jnp.exp2((v - top) * LOG2E) for v in z])
+                tot = functools.reduce(jnp.add, [jnp.exp2(v - top) for v in z])
                 picked = functools.reduce(jnp.add, [jnp.where(m, v, 0.0) for m, v in zip(masks, z)])
                 row_top = jnp.max(top, axis=1, keepdims=True)
-                row_tot = jnp.sum(tot * jnp.exp2((top - row_top) * LOG2E), axis=1, keepdims=True)
-                norm = row_top * LOG2E + jnp.log2(row_tot)
-                blank = z[0][:, 0:1] * LOG2E - norm
-                label = jnp.sum(picked, axis=1, keepdims=True) * LOG2E - norm
+                row_tot = jnp.sum(tot * jnp.exp2(top - row_top), axis=1, keepdims=True)
+                norm = row_top + jnp.log2(row_tot)
+                blank = z[0][:, 0:1] - norm
+                label = jnp.sum(picked, axis=1, keepdims=True) - norm
                 cur = jnp.where(lane == utt + 32 * k, blank, cur)
                 cur = jnp.where(lane == utt + 32 * k + 16, label, cur)
                 norm_out[ug * T_LOC + t] = jnp.where(lane == utt, norm, norm_out[ug * T_LOC + t])
@@ -102,7 +102,7 @@
     def utterance(n_grp):
         h_out[0] = h_next[...]
         for ug in range(n_grp):
-            z = dot(h_out[ug] if ug else h_next[...], w_out[...])
+            z = dot(h_out[ug] if ug else h_next[...], w_out[...]) * LOG2E
             z_out[ug] = z
             if ug == 0:
                 soften(step - 1, last_of(jnp.maximum(step - 1, 0)), z_last)
@@ -167,17 +167,17 @@
 
 def lattice_kernel(stat, norm, flen, llen, q0_out, q1_out, norm_out, loss_out, gath, s_blank, s_label, s_alpha, s_beta, send_sem, recv_sem):
     me = lax.axis_index("seq")
+    mate = me + 1 - 2 * lax.rem(me, 2)
+    across = lax.rem(me + 2, N_SEQ)
     barrier = pltpu.get_barrier_semaphore()
-    for off in range(1, N_SEQ):
-        pl.semaphore_signal(barrier, inc=1, device_id={"seq": lax.rem(me + off, N_SEQ)}, device_id_type=MESH)
-    pl.semaphore_wait(barrier, N_SEQ - 1)
-    copies = []
-    for off in range(1, N_SEQ):
-        cp = pltpu.make_async_remote_copy(
-            src_ref=stat, dst_ref=gath.at[off - 1], send_sem=send_sem.at[off - 1], recv_sem=recv_sem.at[off - 1],
-            device_id={"seq": lax.rem(me + off, N_SEQ)}, device_id_type=MESH)
-        cp.start()
-        copies.append(cp)
+    for dev in (mate, across):
+        pl.semaphore_signal(barrier, inc=1, device_id={"seq": dev}, device_id_type=MESH)
+    pl.semaphore_wait(barrier, 2)
+    copies = [pltpu.make_async_remote_copy(src_ref=src, dst_ref=gath.at[k], send_sem=send_sem.at[k], recv_sem=recv_sem.at[k],
+                                           device_id={"seq": dev}, device_id_type=MESH)
+              for k, (src, dev) in enumerate(((stat, across), (stat, mate), (gath.at[0], mate)))]
+    copies[0].start()
+    copies[1].start()
 
     sub = lax.broadcasted_iota(jnp.int32, (SUB, LANES), 0)
     sub24 = lax.broadcasted_iota(jnp.int32, (N_UP, LANES), 0)
@@ -216,9 +216,13 @@
                     s_label[pl.ds(t * N_UP + 200 * ug, SUB, stride=25), :] = jnp.where(ok & in_l, la, NEG)
 
     place(stat, me)
-    for off in range(1, N_SEQ):
-        copies[off - 1].wait_recv()
-        place(gath.at[off - 1], lax.rem(me + N_SEQ - off, N_SEQ))
+    copies[1].wait_recv()
+    place(gath.at[1], mate)
+    copies[0].wait_recv()
+    copies[2].start()
+    place(gath.at[0], across)
+    copies[2].wait_recv()
+    place(gath.at[2], lax.rem(mate + 2, N_SEQ))
 
     alpha0 = jnp.where(sub24 == 0, 0.0, NEG)
     s_alpha[pl.ds(0, N_UP), :] = alpha0
@@ -487,11 +491,11 @@
 
     @pl.when(step == 0)
     def _():
-        links.greet()
-        far().start()
         for utt in range(RING - 1):
             z_copy(utt).start()
             h_copy(utt).start()
+        links.greet()
+        far().start()
         w_out_t[:, :n_j] = w_out[...].T
         w_out_t[:, n_j:] = jnp.zeros((n_v, w_out_t.shape[1] - n_j), BF16)
 
@@ -507,7 +511,7 @@
                 tiles = []
                 for k in range(n_v // LANES):
                     z = z_ring[z_slot, ug, row:row + SUB, k * LANES:k * LANES + LANES]
-                    g = jnp.exp2(z * LOG2E - norm) - jnp.where(masks[k], q1, 0.0)
+                    g = jnp.exp2(z - norm) - jnp.where(masks[k], q1, 0.0)
                     tiles.append(g - jnp.where(lane == 0, q0, 0.0) if k == 0 else g)
                 pair.append(jnp.concatenate(tiles, axis=1))
             rows = pl.ds(pl.multiple_of(step * utt_rows + ug * ROWS + t * SUB, 16), 16)
@@ -522,13 +526,13 @@
             ds = dhs[ug][t * SUB:t * SUB + 16, :] * (1.0 - hid * hid)
             both = ds[:SUB] + ds[SUB:]
             dc = both if dc is None else dc + both
-            if ug > 0:
-                ds = ds + da_part[t * SUB:t * SUB + 16, :]
-            if ug < UG - 1:
-                da_part[t * SUB:t * SUB + 16, :] = ds
-            else:
-                for k in range(2):
-                    da_all[pl.ds(utt * T_LOC + t + k, 1), :] = jnp.sum(ds[SUB * k:SUB * k + SUB], axis=0, keepdims=True)
+            here = slice(t * SUB, t * SUB + 2 * SUB)
+            for c in range(n_j // LANES):
+                tile = ds[:, c * LANES:c * LANES + LANES]
+                da_part[c, here, :] = tile + da_part[c, here, :] if ug else tile
+        if ug == UG - 1:
+            sums = [functools.reduce(jnp.add, [da_part[c, pl.ds(k, T_LOC, stride=SUB), :] for k in range(SUB)]) for c in range(n_j // LANES)]
+            da_all[pl.ds(pl.multiple_of(utt * T_LOC, SUB), T_LOC), :] = jnp.concatenate(sums, axis=1)
         dc_out[pl.ds(pl.multiple_of(utt * N_UP + ug * SUB, SUB), SUB), :] = dc
 
     @pl.when(step + RING - 1 < N_UTT)
@@ -627,7 +631,7 @@
         ],
         scratch_shapes=[
             pltpu.VMEM((n_cell, n_v), BF16), pltpu.VMEM((n_cell, n_j), BF16), pltpu.VMEM((N_UTT * T_LOC, n_j), F32),
-            pltpu.VMEM((ROWS, n_j), F32),
+            pltpu.VMEM((n_j // LANES, ROWS, LANES), F32),
             *[pltpu.VMEM((ROWS, n_v), BF16)] * 3, *[pltpu.VMEM((ROWS, n_j), F32)] * 3,
             pltpu.VMEM((n_v, n_j + (-n_j) % 256), BF16), pltpu.VMEM((RING, UG, ROWS, n_v), F32),
             pltpu.VMEM((n_j, n_v), F32), pltpu.VMEM((n_j, n_v), F32), pltpu.VMEM((n_dc, n_j), F32),
@@ -645,8 +649,8 @@
 def finish_kernel(loss, *refs):
     ins, o_loss, outs = refs[:FIN_IN], refs[FIN_IN], refs[FIN_IN + 1:FIN_IN + 1 + FIN_OUT]
     bufs, vals, in_sem, out_sem = refs[FIN_IN + 1 + FIN_OUT:-FIN_OUT - 2], refs[-FIN_OUT - 2:-2], refs[-2], refs[-1]
-    g_out, g_enc, da, w_enc, g_dc, w_pred, pred, pred_far = bufs
-    v_wout, v_wenc, v_enc, v_pred, v_wpred = vals
+    g_dc, pred, pred_far, g_out, g_enc, w_pred, da, w_enc = bufs
+    v_wpred, v_wout, v_wenc, v_pred, v_enc = vals
     loads = [pltpu.make_async_copy(src, dst, in_sem.at[k]) for k, (src, dst) in enumerate(zip(ins, bufs))]
     stores = [pltpu.make_async_copy(src, dst, out_sem.at[k]) for k, (src, dst) in enumerate(zip(vals, outs))]
     for cp in loads:
@@ -654,25 +658,24 @@
     y = lax.axis_index("data")
     n_r = pred.shape[0]
     o_loss[...] = loss[0:1, :N_UTT]
-    loads[0].wait()
-    v_wout[...] = g_out[...].astype(F32)
-    stores[0].start()
-    loads[1].wait()
-    v_wenc[...] = g_enc[...].astype(F32).T
-    stores[1].start()
-    loads[2].wait()
-    loads[3].wait()
-    v_enc[...] = dot(da[...], w_enc[...], ((1,), (1,))).astype(BF16)
-    stores[2].start()
-    loads[4].wait()
-    loads[5].wait()
+    for k in range(3):
+        loads[k].wait()
     dc_own = g_dc[rows_at(y * n_r, n_r), :]
     dc_far = g_dc[rows_at((1 - y) * n_r, n_r), :]
+    v_wpred[...] = dot(pred[...], dc_own, ((0,), (0,))) + dot(pred_far[...], dc_far, ((0,), (0,)))
+    stores[0].start()
+    loads[3].wait()
+    v_wout[...] = g_out[...].astype(F32)
+    stores[1].start()
+    loads[4].wait()
+    v_wenc[...] = g_enc[...].astype(F32).T
+    stores[2].start()
+    loads[5].wait()
     v_pred[...] = dot(dc_own, w_pred[...], ((1,), (1,)))
     stores[3].start()
     loads[6].wait()
     loads[7].wait()
-    v_wpred[...] = dot(pred[...], dc_own, ((0,), (0,))) + dot(pred_far[...], dc_far, ((0,), (0,)))
+    v_enc[...] = dot(da[...], w_enc[...], ((1,), (1,))).astype(BF16)
     stores[4].start()
     for cp in stores:
         cp.wait()
@@ -685,9 +688,9 @@
 def finish(loss, g_enc, g_out, g_dc, pred, pred_far, w_pred, da, w_enc):
     vm = pl.BlockSpec(memory_space=pltpu.VMEM)
     hbm = pl.BlockSpec(memory_space=pl.ANY)
-    ins = (g_out, g_enc, da, w_enc, g_dc, w_pred, pred, pred_far)
-    outs = [(g_out.shape, F32), (w_enc.shape, F32), (pred.shape, BF16), (pred.shape, F32), (w_pred.shape, F32)]
-    loss, grad_w_out, grad_w_enc, grad_enc, grad_pred, grad_w_pred = pl.pallas_call(
+    ins = (g_dc, pred, pred_far, g_out, g_enc, w_pred, da, w_enc)
+    outs = [(w_pred.shape, F32), (g_out.shape, F32), (w_enc.shape, F32), (pred.shape, F32), (pred.shape, BF16)]
+    loss, grad_w_pred, grad_w_out, grad_w_enc, grad_pred, grad_enc = pl.pallas_call(
         finish_kernel,
         in_specs=[vm] + [hbm] * FIN_IN,
         out_specs=[vm] + [hbm] * FIN_OUT,

time: 116 us -> 114 us (0.983)
  Pallas kernels: 116 us -> 114 us
    pallas_call x1, Pallas kernels: 69.5 us -> 67.9 us  [joint_backward(): pl.pallas_call(backward_kernel, grid=(N_UTT + 1 + n_v // W_CHUNK,), in_sp...]
    pallas_call x1, Pallas kernels: 9.99 us -> 8.53 us  [finish(): pl.pallas_call(finish_kernel, in_specs=[vm] + [hbm] * FIN_IN, out_specs=[...]
where the time goes in v5:
time: 114 us; the launch traced here: 115 us
  Pallas kernels  114 us (100%)
    pallas_call x1, Pallas kernels, joint_backward(): pl.pallas_call(backward_kernel, grid=(N_UTT + 1 + n_v // W_CHUNK,), in_sp...  67.9 us
    pallas_call x1, Pallas kernels, joint_forward(): pl.pallas_call(forward_kernel, grid=(N_UTT,), in_specs=[pl.BlockSpec(memo...  25.6 us
    pallas_call x1, Pallas kernels, lattice(): pl.pallas_call(lattice_kernel, in_specs=[vm] * 2 + [pl.BlockSpec(memory_s...  11.8 us
    pallas_call x1, Pallas kernels, finish(): pl.pallas_call(finish_kernel, in_specs=[vm] + [hbm] * FIN_IN, out_specs=[...  8.53 us

profile of v5, /device:TPU:0, one launch (start us, length us, event | category | flops | bytes accessed | tf_op | source)
XLA Modules:
  0.0 114.6 jit_solution(17755446565156896547)
XLA Ops:
  0.6 25.6 %joint_forward.1 = (f32[16,3,192,1024]{3,2,1,0:T(8,128)}, bf16[16,3,192,640]{3,2,1,0:T(8,128)(2,1)}, f32[18,8,128]{2,1,0:T(8,128)}, f32[72,8,128]{2,1,0:T(8,128)}) custom-call(s32[16,23]{1,0:T(8,128)} %labels.3, s32[16]{0:T(128)} %llen.3, bf16[384,1024]{1,0:T(8,128)(2,1)} %bitcast.10, bf16[384,1024]{1,0:T(8,128)(2,1)} %bitcast.7, bf16[1024,640]{1,0:T(8,128)(2,1)} %refs_7_.1, ...), custom_call_target="tpu_custom_call" | custom-call | tf_op jit(solution)/shard_map/joint_forward/pallas_call | solution.py:140
  26.2 11.8 %lattice.1 = (f32[72,8,128]{2,1,0:T(8,128)}, f32[72,8,128]{2,1,0:T(8,128)}, f32[72,8,128]{2,1,0:T(8,128)}, f32[8,128]{1,0:T(8,128)}) custom-call(f32[18,8,128]{2,1,0:T(8,128)} %get-tuple-element.25.stat, f32[72,8,128]{2,1,0:T(8,128)} %get-tuple-element.26.norm, s32[16]{0:T(128)} %flen.1, s32[16]{0:T(128)} %llen.3), custom_call_target="tpu_custom_call" | custom-call | tf_op jit(solution)/shard_map/lattice/pallas_call | solution.py:271
  38.0 67.9 %joint_backward.1 = (bf16[384,640]{1,0:T(8,128)(2,1)}, bf16[640,1024]{1,0:T(8,128)(2,1)}, bf16[640,1024]{1,0:T(8,128)(2,1)}, bf16[768,640]{1,0:T(8,128)(2,1)}, bf16[384,1024]{1,0:T(8,128)(2,1)}) custom-call(s32[16,23]{1,0:T(8,128)} %labels.3, bf16[384,1024]{1,0:T(8,128)(2,1)} %bitcast.8, f32[16,3,192,1024]{3,2,1,0:T(8,128)} %get-tuple-element.28.z_hbm, ...), custom_call_target="tpu_custom_call" | custom-call | tf_op jit(solution)/shard_map/joint_backward/pallas_call | solution.py:616
  105.9 8.5 %finish.1 = (f32[1,16]{1,0:T(1,128)}, f32[1024,640]{1,0:T(8,128)}, f32[640,1024]{1,0:T(8,128)}, f32[1024,640]{1,0:T(8,128)}, f32[384,1024]{1,0:T(8,128)}, /*index=5*/bf16[384,1024]{1,0:T(8,128)(2,1)}) custom-call(f32[8,128]{1,0:T(8,128)} %get-tuple-element.27.loss, bf16[768,640]{1,0:T(8,128)(2,1)} %get-tuple-element.33.refs_0_, bf16[384,1024]{1,0:T(8,128)(2,1)} %bitcast.9, ...), custom_call_target="tpu_custom_call" | custom-call | tf_op jit(solution)/shard_map/finish/pallas_call | solution.py:693

commit v6 on v5

--- a/solution.py
+++ b/solution.py
@@ -23,6 +23,7 @@
 N_SEQ = 4
 T_ALL = T_LOC * N_SEQ
 RING = 4
+B_RING = 3
 N_DIAG = T_ALL + N_UP - 1
 ROWS = SUB * T_LOC
 
@@ -165,20 +166,11 @@
     return jnp.maximum(x, y) + jnp.log2(1.0 + jnp.exp2(-jnp.abs(x - y)))
 
 
-def lattice_kernel(stat, norm, flen, llen, q0_out, q1_out, norm_out, loss_out, gath, s_blank, s_label, s_alpha, s_beta, send_sem, recv_sem):
-    me = lax.axis_index("seq")
-    mate = me + 1 - 2 * lax.rem(me, 2)
+def run_lattice(links, moves, stat, norm, flen, llen, q0_out, q1_out, norm_out, loss_out, gath, s_blank, s_label, s_alpha, s_beta):
+    me = links.seq
+    mate = me + 1 - 2 * links.core
     across = lax.rem(me + 2, N_SEQ)
-    barrier = pltpu.get_barrier_semaphore()
-    for dev in (mate, across):
-        pl.semaphore_signal(barrier, inc=1, device_id={"seq": dev}, device_id_type=MESH)
-    pl.semaphore_wait(barrier, 2)
-    copies = [pltpu.make_async_remote_copy(src_ref=src, dst_ref=gath.at[k], send_sem=send_sem.at[k], recv_sem=recv_sem.at[k],
-                                           device_id={"seq": dev}, device_id_type=MESH)
-              for k, (src, dev) in enumerate(((stat, across), (stat, mate), (gath.at[0], mate)))]
-    copies[0].start()
-    copies[1].start()
-
+    row_x, row_core, row_relay = moves
     sub = lax.broadcasted_iota(jnp.int32, (SUB, LANES), 0)
     sub24 = lax.broadcasted_iota(jnp.int32, (N_UP, LANES), 0)
     lane = lax.broadcasted_iota(jnp.int32, (SUB, LANES), 1)
@@ -195,11 +187,11 @@
         s_label[pl.ds(pl.multiple_of(i * SUB, SUB), SUB), :] = jnp.full((SUB, LANES), NEG, F32)
         return c
 
-    lax.fori_loop(0, n_pad // SUB, fill, 0, unroll=SUB)
+    lax.fori_loop(0, n_pad // SUB, fill, 0, unroll=11)
     end_grp = [jnp.where(sub + SUB * ug == ub, 0.0, NEG) for ug in range(UG)]
-    for t in range(T_ALL, T_ALL + N_UP):
+    for d in range(T_ALL, N_DIAG + 2):
         for ug in range(UG):
-            s_blank[pl.ds(t * N_UP + 200 * ug, SUB, stride=25), :] = end_grp[ug]
+            s_blank[d * N_UP + SUB * ug:d * N_UP + SUB * ug + SUB, :] = end_grp[ug]
 
     def place(src, src_seq):
         for t4 in range(T_LOC // 4):
@@ -216,12 +208,12 @@
                     s_label[pl.ds(t * N_UP + 200 * ug, SUB, stride=25), :] = jnp.where(ok & in_l, la, NEG)
 
     place(stat, me)
-    copies[1].wait_recv()
+    row_core().wait_recv()
     place(gath.at[1], mate)
-    copies[0].wait_recv()
-    copies[2].start()
+    row_x().wait_recv()
+    row_relay().start()
     place(gath.at[0], across)
-    copies[2].wait_recv()
+    row_relay().wait_recv()
     place(gath.at[2], lax.rem(mate + 2, N_SEQ))
 
     alpha0 = jnp.where(sub24 == 0, 0.0, NEG)
@@ -261,23 +253,6 @@
             q0_out[idx] = q0
             q1_out[idx] = q1
             norm_out[idx] = norm[idx] - jnp.log2(q0 + q1)
-    for cp in copies:
-        cp.wait_send()
-
-
-def lattice(stat, norm, flen, llen):
-    vm = pl.BlockSpec(memory_space=pltpu.VMEM)
-    n_rows = (T_ALL + 2 * N_UP) * N_UP
-    return pl.pallas_call(
-        lattice_kernel,
-        in_specs=[vm] * 2 + [pl.BlockSpec(memory_space=pltpu.SMEM)] * 2,
-        out_specs=[vm] * 4,
-        out_shape=[jax.ShapeDtypeStruct((UG * T_LOC, SUB, LANES), F32)] * 3 + [jax.ShapeDtypeStruct((SUB, LANES), F32)],
-        scratch_shapes=[pltpu.VMEM((N_SEQ - 1,) + stat.shape, F32)] + [pltpu.VMEM((n_rows, LANES), F32)] * 4
-        + [pltpu.SemaphoreType.DMA((N_SEQ - 1,)), pltpu.SemaphoreType.DMA((N_SEQ - 1,))],
-        compiler_params=pltpu.CompilerParams(collective_id=0, has_side_effects=True),
-        name="lattice",
-    )(stat, norm, flen, llen)
 
 
 class Links:
@@ -287,6 +262,7 @@
         self.core = lax.rem(seq, 2)
         self.x = lax.div(seq, 2)
         self.y = lax.axis_index("data")
+        self.seq = seq
         self.dev = {
             "core": {"seq": seq + 1 - 2 * self.core},
             "x": {"seq": lax.rem(seq + 2, N_SEQ)},
@@ -445,7 +421,7 @@
     return [s1, s2, s3, s4, s5, s6]
 
 
-N_COPY = 10 * 5 + 1
+N_COPY = 10 * 5 + 4
 
 
 def sum_scratch(n_row, n_col):
@@ -456,10 +432,10 @@
 W_CHUNK = 256
 
 
-def backward_kernel(labels, pred, z_hbm, h_hbm, q0_ref, q1_ref, norm_ref, w_out, enc, da_out, g_enc_out, g_out_out, g_dc_out, far_out,
+def backward_kernel(labels, flen, llen, stat, norm, pred, z_hbm, h_hbm, w_out, enc, loss_out, da_out, g_enc_out, g_out_out, g_dc_out, far_out,
                     dz_all, h_all, da_all, da_part, dz0, dz1, dz2, dh0, dh1, dh2, w_out_t, z_ring, dw_enc, dw_out, dc_out, g_enc, g_out, g_dc,
                     es0, es1, es2, er0, er1, er2, ps0, ps1, ps2, pr0, pr1, pr2, qs0, qs1, qs2, qr0, qr1, qr2, rs0, rs1, rs2, rr0, rr1, rr2, ds0, ds1, dr0, dr1,
-                    h_sem, z_sem, o_sem, send_sem, recv_sem):
+                    q0_ref, q1_ref, norm_ref, gath, s_blank, s_label, s_alpha, s_beta, h_sem, z_sem, o_sem, w_sem, send_sem, recv_sem):
     step = pl.program_id(0)
     lane = lax.broadcasted_iota(jnp.int32, (SUB, LANES), 1)
     sub = lax.broadcasted_iota(jnp.int32, (SUB, LANES), 0)
@@ -468,7 +444,7 @@
 
     dzs, dhs = (dz0, dz1, dz2), (dh0, dh1, dh2)
     prev = jnp.maximum(step - 1, 0)
-    z_slot = lax.rem(step, RING)
+    z_slot = lax.rem(step, B_RING)
 
     def multiply(ug):
         dhs[ug][...] = dot(dzs[ug][...], w_out_t[...])[:, :n_j]
@@ -478,11 +454,18 @@
         return pltpu.make_async_copy(h_hbm.at[rows, :], h_all.at[rows, :], h_sem.at[utt])
 
     def z_copy(utt):
-        slot = lax.rem(utt, RING)
+        slot = lax.rem(utt, B_RING)
         return pltpu.make_async_copy(z_hbm.at[utt], z_ring.at[slot], z_sem.at[slot])
 
     links = Links(send_sem, recv_sem)
     far = links.copy(lambda: (pred, far_out), "y")
+    moves = (links.copy(lambda: (stat, gath.at[0]), "x"), links.copy(lambda: (stat, gath.at[1]), "core"),
+             links.copy(lambda: (gath.at[0], gath.at[2]), "core"))
+    n_enc = enc.shape[0]
+
+    def weight_copies():
+        return (pltpu.make_async_copy(w_out, dz_all.at[dz_all.shape[0] - n_j:, :], w_sem.at[0]),
+                pltpu.make_async_copy(enc, g_out.at[:n_enc, :], w_sem.at[1]))
     e_st = sum_stages(links, dw_enc, g_enc, (es0, es1, es2), (er0, er1, er2), 0, n_v)
     p_st = sum_stages(links, dw_out, g_out, (ps0, ps1, ps2), (pr0, pr1, pr2), 0, n_v // 2)
     q_st = sum_stages(links, dw_out, g_out, (qs0, qs1, qs2), (qr0, qr1, qr2), n_v // 2, n_v // 4)
@@ -491,13 +474,19 @@
 
     @pl.when(step == 0)
     def _():
-        for utt in range(RING - 1):
+        for utt in range(B_RING - 1):
             z_copy(utt).start()
             h_copy(utt).start()
+        for cp in weight_copies():
+            cp.start()
         links.greet()
+        moves[0]().start()
+        moves[1]().start()
         far().start()
-        w_out_t[:, :n_j] = w_out[...].T
+        weight_copies()[0].wait()
+        w_out_t[:, :n_j] = dz_all[dz_all.shape[0] - n_j:, :].T
         w_out_t[:, n_j:] = jnp.zeros((n_v, w_out_t.shape[1] - n_j), BF16)
+        run_lattice(links, moves, stat, norm, flen, llen, q0_ref, q1_ref, norm_ref, loss_out, gath, s_blank, s_label, s_alpha, s_beta)
 
     def logit_grads(ug):
         shift = LANES - step
@@ -535,10 +524,10 @@
             da_all[pl.ds(pl.multiple_of(utt * T_LOC, SUB), T_LOC), :] = jnp.concatenate(sums, axis=1)
         dc_out[pl.ds(pl.multiple_of(utt * N_UP + ug * SUB, SUB), SUB), :] = dc
 
-    @pl.when(step + RING - 1 < N_UTT)
-    def _():
-        z_copy(step + RING - 1).start()
-        h_copy(step + RING - 1).start()
+    @pl.when(step + B_RING - 1 < N_UTT)
+    def _():
+        z_copy(step + B_RING - 1).start()
+        h_copy(step + B_RING - 1).start()
 
     @pl.when(step < N_UTT)
     def _():
@@ -561,7 +550,8 @@
         hidden_grads(prev, 2)
         da = da_all[...].astype(BF16)
         da_out[...] = da
-        dw_enc[...] = dot(da, enc[...], ((0,), (0,)))
+        weight_copies()[1].wait()
+        dw_enc[...] = dot(da, g_out[:n_enc, :], ((0,), (0,)))
         e_st[0]()
         c_st[0]()
 
@@ -608,7 +598,7 @@
         out_out.wait()
 
 
-def joint_backward(labels, pred, z, h, q0, q1, norm, w_out, enc):
+def joint_backward(labels, flen, llen, stat, norm, pred, z, h, w_out, enc):
     n_j, n_v = w_out.shape
     n_cell = N_UTT * UG * ROWS
     n_dc = N_UTT * N_UP
@@ -616,13 +606,10 @@
     return pl.pallas_call(
         backward_kernel,
         grid=(N_UTT + 1 + n_v // W_CHUNK,),
-        in_specs=[
-            pl.BlockSpec(memory_space=pltpu.SMEM),
-            *[pl.BlockSpec(memory_space=pl.ANY)] * 3,
-            full(q0.shape), full(q1.shape), full(norm.shape), full(w_out.shape), full(enc.shape),
-        ],
-        out_specs=[full((N_UTT * T_LOC, n_j))] + [pl.BlockSpec(memory_space=pl.ANY)] * 4,
+        in_specs=[pl.BlockSpec(memory_space=pltpu.SMEM)] * 3 + [full(stat.shape), full(norm.shape)] + [pl.BlockSpec(memory_space=pl.ANY)] * 5,
+        out_specs=[full((SUB, LANES)), full((N_UTT * T_LOC, n_j))] + [pl.BlockSpec(memory_space=pl.ANY)] * 4,
         out_shape=[
+            jax.ShapeDtypeStruct((SUB, LANES), F32),
             jax.ShapeDtypeStruct((N_UTT * T_LOC, n_j), BF16),
             jax.ShapeDtypeStruct((n_j, n_v), BF16),
             jax.ShapeDtypeStruct((n_j, n_v), BF16),
@@ -633,17 +620,19 @@
             pltpu.VMEM((n_cell, n_v), BF16), pltpu.VMEM((n_cell, n_j), BF16), pltpu.VMEM((N_UTT * T_LOC, n_j), F32),
             pltpu.VMEM((n_j // LANES, ROWS, LANES), F32),
             *[pltpu.VMEM((ROWS, n_v), BF16)] * 3, *[pltpu.VMEM((ROWS, n_j), F32)] * 3,
-            pltpu.VMEM((n_v, n_j + (-n_j) % 256), BF16), pltpu.VMEM((RING, UG, ROWS, n_v), F32),
+            pltpu.VMEM((n_v, n_j + (-n_j) % 256), BF16), pltpu.VMEM((B_RING, UG, ROWS, n_v), F32),
             pltpu.VMEM((n_j, n_v), F32), pltpu.VMEM((n_j, n_v), F32), pltpu.VMEM((n_dc, n_j), F32),
             pltpu.VMEM((n_j, n_v), BF16), pltpu.VMEM((n_j, n_v), BF16), pltpu.VMEM((2 * n_dc, n_j), BF16),
             *sum_scratch(n_j, n_v) * 2, *sum_scratch(n_j, n_v // 2) * 2, *sum_scratch(n_j, n_v // 4) * 4,
             *[pltpu.VMEM((n_dc // 2, n_j), BF16), pltpu.VMEM((n_dc // 4, n_j), BF16)] * 2,
-            pltpu.SemaphoreType.DMA((N_UTT,)), pltpu.SemaphoreType.DMA((RING,)), pltpu.SemaphoreType.DMA((3,)),
+            *[pltpu.VMEM(norm.shape, F32)] * 3, pltpu.VMEM((N_SEQ - 1,) + stat.shape, F32),
+            *[pltpu.VMEM(((N_DIAG + 2) * N_UP, LANES), F32)] * 4,
+            pltpu.SemaphoreType.DMA((N_UTT,)), pltpu.SemaphoreType.DMA((B_RING,)), pltpu.SemaphoreType.DMA((3,)), pltpu.SemaphoreType.DMA((2,)),
             pltpu.SemaphoreType.DMA((N_COPY,)), pltpu.SemaphoreType.DMA((N_COPY,)),
         ],
         compiler_params=pltpu.CompilerParams(collective_id=1, has_side_effects=True, vmem_limit_bytes=VMEM_FULL),
         name="joint_backward",
-    )(labels, pred, z, h.reshape(n_cell, n_j), q0, q1, norm, w_out, enc)
+    )(labels, flen, llen, stat, norm, pred, z, h.reshape(n_cell, n_j), w_out, enc)
 
 
 def finish_kernel(loss, *refs):
@@ -716,8 +705,7 @@
         enc2 = enc_loc.reshape(N_UTT * T_LOC, n_h)
         pred2 = pred_loc.reshape(N_UTT * N_UP, n_h)
         z, h, stat, norm = joint_forward(labels, label_len, enc2, pred2, w_enc, w_pred, w_out)
-        q0, q1, norm, loss = lattice(stat, norm, frame_len, label_len)
-        da, g_enc, g_out, g_dc, pred_far = joint_backward(labels, pred2, z, h, q0, q1, norm, w_out, enc2)
+        loss, da, g_enc, g_out, g_dc, pred_far = joint_backward(labels, frame_len, label_len, stat, norm, pred2, z, h, w_out, enc2)
         loss, grad_enc, grad_pred, grad_w_enc, grad_w_pred, grad_w_out = finish(loss, g_enc, g_out, g_dc, pred2, pred_far, w_pred, da, w_enc)
         return loss.reshape(N_UTT), grad_enc.reshape(enc_loc.shape), grad_pred.reshape(pred_loc.shape), grad_w_enc, grad_w_pred, grad_w_out
 

time: 114 us -> 110 us (0.965)
  Pallas kernels: 114 us -> 109 us
    pallas_call x1 -> x0, Pallas kernels: 11.8 us -> none  [lattice(): pl.pallas_call(lattice_kernel, in_specs=[vm] * 2 + [pl.BlockSpec(memory_s...]
    pallas_call x1, Pallas kernels: 67.9 us -> 74.5 us  [joint_backward(): pl.pallas_call(backward_kernel, grid=(N_UTT + 1 + n_v // W_CHUNK,), in_sp...]
where the time goes in v6:
time: 110 us
  Pallas kernels  109 us (99%)
    pallas_call x1, Pallas kernels, joint_backward(): pl.pallas_call(backward_kernel, grid=(N_UTT + 1 + n_v // W_CHUNK,), in_sp...  74.5 us
    pallas_call x1, Pallas kernels, joint_forward(): pl.pallas_call(forward_kernel, grid=(N_UTT,), in_specs=[pl.BlockSpec(memo...  26.4 us
    pallas_call x1, Pallas kernels, finish(): pl.pallas_call(finish_kernel, in_specs=[vm] + [hbm] * FIN_IN, out_specs=[...  8.53 us

profile of v6, /device:TPU:0, one launch (start us, length us, event | category | flops | bytes accessed | tf_op | source)
XLA Modules:
  0.0 110.2 jit_solution(9104565530383349500)
XLA Ops:
  0.6 26.4 %joint_forward.1 = (f32[16,3,192,1024]{3,2,1,0:T(8,128)}, bf16[16,3,192,640]{3,2,1,0:T(8,128)(2,1)}, f32[18,8,128]{2,1,0:T(8,128)}, f32[72,8,128]{2,1,0:T(8,128)}) custom-call(s32[16,23]{1,0:T(8,128)} %labels.3, s32[16]{0:T(128)} %llen.3, bf16[384,1024]{1,0:T(8,128)(2,1)} %bitcast.10, bf16[384,1024]{1,0:T(8,128)(2,1)} %bitcast.7, bf16[1024,640]{1,0:T(8,128)(2,1)} %refs_7_.1, ...), custom_call_target="tpu_custom_call" | custom-call | tf_op jit(solution)/shard_map/joint_forward/pallas_call | solution.py:141
  27.0 74.5 %joint_backward.1 = (f32[8,128]{1,0:T(8,128)}, bf16[384,640]{1,0:T(8,128)(2,1)}, bf16[640,1024]{1,0:T(8,128)(2,1)}, bf16[640,1024]{1,0:T(8,128)(2,1)}, bf16[768,...) custom-call(s32[16,23]{1,0:T(8,128)} %labels.3, s32[16]{0:T(128)} %flen.1, s32[16]{0:T(128)} %llen.3, ...), custom_call_target="tpu_custom_call" | custom-call | tf_op jit(solution)/shard_map/joint_backward/pallas_call | solution.py:606
  101.5 8.5 %finish.1 = (f32[1,16]{1,0:T(1,128)}, f32[1024,640]{1,0:T(8,128)}, f32[640,1024]{1,0:T(8,128)}, f32[1024,640]{1,0:T(8,128)}, f32[384,1024]{1,0:T(8,128)}, /*index=5*/bf16[384,1024]{1,0:T(8,128)(2,1)}) custom-call(f32[8,128]{1,0:T(8,128)} %get-tuple-element.26.loss, bf16[768,640]{1,0:T(8,128)(2,1)} %get-tuple-element.27.refs_0_, bf16[384,1024]{1,0:T(8,128)(2,1)} %bitcast.9, ...), custom_call_target="tpu_custom_call" | custom-call | tf_op jit(solution)/shard_map/finish/pallas_call | solution.py:682

commit v7 on v6

--- a/solution.py
+++ b/solution.py
@@ -543,59 +543,67 @@
         logit_grads(2)
         hidden_grads(step, 0)
 
-    @pl.when(step == N_UTT)
+    @pl.when(step >= N_UTT)
     def _():
-        multiply(2)
-        hidden_grads(prev, 1)
-        hidden_grads(prev, 2)
-        da = da_all[...].astype(BF16)
-        da_out[...] = da
-        weight_copies()[1].wait()
-        dw_enc[...] = dot(da, g_out[:n_enc, :], ((0,), (0,)))
-        e_st[0]()
-        c_st[0]()
-
-    plan = [
-        ((c_st[1], e_st[1]), ()),
-        ((), (c_st[2], p_st[0])),
-        ((e_st[2], p_st[1]), ()),
-        ((e_st[3], q_st[0]), (
-            r_st[0], p_st[2], q_st[1], r_st[1], c_st[3], p_st[3], r_st[2], q_st[2], e_st[4], c_st[4], q_st[3], r_st[3], p_st[4],
-            q_st[4], r_st[4], p_st[5], e_st[5], q_st[5])),
-    ]
-    for part, (lo, hi) in enumerate(((0, 3 * LANES), (3 * LANES, n_j))):
-        @pl.when(step > N_UTT)
-        def _(lo=lo, hi=hi):
-            cols = pl.ds(pl.multiple_of((step - N_UTT - 1) * W_CHUNK, W_CHUNK), W_CHUNK)
-            dw_out[lo:hi, cols] = dot(h_all[:, lo:hi], dz_all[:, cols], ((0,), (0,)))
-
-        for n, stages in enumerate(plan):
-            if stages[part]:
-                @pl.when(step == N_UTT + 1 + n)
-                def _(stages=stages[part]):
-                    for stage in stages:
-                        stage()
-
-    @pl.when(step == N_UTT + len(plan))
-    def _():
-        p_st[6]()
-        r_st[5]()
-        r_st[6]()
-        e_st[6]()
-        out_enc = pltpu.make_async_copy(g_enc, g_enc_out, o_sem.at[1])
-        out_enc.start()
-        q_st[6]()
-        out_out = pltpu.make_async_copy(g_out, g_out_out, o_sem.at[2])
-        out_out.start()
-        c_st[5]()
-        out_dc = pltpu.make_async_copy(g_dc, g_dc_out, o_sem.at[0])
-        out_dc.start()
-        far().wait_recv()
-        for cp in links.copies:
-            cp().wait_send()
-        out_dc.wait()
-        out_enc.wait()
-        out_out.wait()
+        @pl.when(step == N_UTT)
+        def _():
+            multiply(2)
+            hidden_grads(prev, 1)
+            hidden_grads(prev, 2)
+            da = da_all[...].astype(BF16)
+            da_out[...] = da
+            weight_copies()[1].wait()
+            dw_enc[...] = dot(da, g_out[:n_enc, :], ((0,), (0,)))
+            e_st[0]()
+            c_st[0]()
+
+        plan = [
+            ((c_st[1], e_st[1]), ()),
+            ((), (c_st[2], p_st[0])),
+            ((e_st[2], p_st[1]), ()),
+            ((e_st[3], q_st[0]), (
+                r_st[0], p_st[2], q_st[1], r_st[1], c_st[3], p_st[3], r_st[2], q_st[2], e_st[4], c_st[4], q_st[3], r_st[3], p_st[4],
+                q_st[4], r_st[4], p_st[5], e_st[5], q_st[5])),
+        ]
+        for part, (lo, hi) in enumerate(((0, 3 * LANES), (3 * LANES, n_j))):
+            @pl.when(step > N_UTT)
+            def _(lo=lo, hi=hi):
+                cols = pl.ds(pl.multiple_of((step - N_UTT - 1) * W_CHUNK, W_CHUNK), W_CHUNK)
+                dw_out[lo:hi, cols] = dot(h_all[:, lo:hi], dz_all[:, cols], ((0,), (0,)))
+
+            for n, stages in enumerate(plan):
+                if stages[part]:
+                    @pl.when(step == N_UTT + 1 + n)
+                    def _(stages=stages[part]):
+                        for stage in stages:
+                            stage()
+
+        @pl.when(step == N_UTT + len(plan))
+        def _():
+            def put(src, dst, k):
+                cp = pltpu.make_async_copy(src, dst, o_sem.at[k])
+                cp.start()
+                return cp
+
+            def put_cols(lo, hi, k):
+                return put(g_out.at[:, lo:hi], g_out_out.at[:, lo:hi], k)
+
+            p_st[6]()
+            puts = [put_cols(0, n_v // 2, 0)]
+            r_st[5]()
+            r_st[6]()
+            puts.append(put_cols(n_v // 2 + n_v // 4, n_v, 1))
+            e_st[6]()
+            puts.append(put(g_enc, g_enc_out, 2))
+            q_st[6]()
+            puts.append(put_cols(n_v // 2, n_v // 2 + n_v // 4, 3))
+            c_st[5]()
+            puts.append(put(g_dc, g_dc_out, 4))
+            far().wait_recv()
+            for cp in links.copies:
+                cp().wait_send()
+            for cp in puts:
+                cp.wait()
 
 
 def joint_backward(labels, flen, llen, stat, norm, pred, z, h, w_out, enc):
@@ -627,7 +635,7 @@
             *[pltpu.VMEM((n_dc // 2, n_j), BF16), pltpu.VMEM((n_dc // 4, n_j), BF16)] * 2,
             *[pltpu.VMEM(norm.shape, F32)] * 3, pltpu.VMEM((N_SEQ - 1,) + stat.shape, F32),
             *[pltpu.VMEM(((N_DIAG + 2) * N_UP, LANES), F32)] * 4,
-            pltpu.SemaphoreType.DMA((N_UTT,)), pltpu.SemaphoreType.DMA((B_RING,)), pltpu.SemaphoreType.DMA((3,)), pltpu.SemaphoreType.DMA((2,)),
+            pltpu.SemaphoreType.DMA((N_UTT,)), pltpu.SemaphoreType.DMA((B_RING,)), pltpu.SemaphoreType.DMA((5,)), pltpu.SemaphoreType.DMA((2,)),
             pltpu.SemaphoreType.DMA((N_COPY,)), pltpu.SemaphoreType.DMA((N_COPY,)),
         ],
         compiler_params=pltpu.CompilerParams(collective_id=1, has_side_effects=True, vmem_limit_bytes=VMEM_FULL),

time: 110 us -> 109 us (level); the launches traced: 110 us -> 108 us
  Pallas kernels: 109 us -> 107 us
    pallas_call x1, Pallas kernels: 26.4 us -> 24.5 us  [joint_forward(): pl.pallas_call(forward_kernel, grid=(N_UTT,), in_specs=[pl.BlockSpec(memo...]
where the time goes in v7:
time: 109 us; the launch traced here: 108 us
  Pallas kernels  107 us (98%)
    pallas_call x1, Pallas kernels, joint_backward(): pl.pallas_call(backward_kernel, grid=(N_UTT + 1 + n_v // W_CHUNK,), in_sp...  73.8 us
    pallas_call x1, Pallas kernels, joint_forward(): pl.pallas_call(forward_kernel, grid=(N_UTT,), in_specs=[pl.BlockSpec(memo...  24.5 us
    pallas_call x1, Pallas kernels, finish(): pl.pallas_call(finish_kernel, in_specs=[vm] + [hbm] * FIN_IN, out_specs=[...  8.53 us

profile of v7, /device:TPU:0, one launch (start us, length us, event | category | flops | bytes accessed | tf_op | source)
XLA Modules:
  0.0 107.7 jit_solution(14777403003969893884)
XLA Ops:
  0.6 24.5 %joint_forward.1 = (f32[16,3,192,1024]{3,2,1,0:T(8,128)}, bf16[16,3,192,640]{3,2,1,0:T(8,128)(2,1)}, f32[18,8,128]{2,1,0:T(8,128)}, f32[72,8,128]{2,1,0:T(8,128)}) custom-call(s32[16,23]{1,0:T(8,128)} %labels.3, s32[16]{0:T(128)} %llen.3, bf16[384,1024]{1,0:T(8,128)(2,1)} %bitcast.10, bf16[384,1024]{1,0:T(8,128)(2,1)} %bitcast.7, bf16[1024,640]{1,0:T(8,128)(2,1)} %refs_7_.1, ...), custom_call_target="tpu_custom_call" | custom-call | tf_op jit(solution)/shard_map/joint_forward/pallas_call | solution.py:141
  25.2 73.8 %joint_backward.1 = (f32[8,128]{1,0:T(8,128)}, bf16[384,640]{1,0:T(8,128)(2,1)}, bf16[640,1024]{1,0:T(8,128)(2,1)}, bf16[640,1024]{1,0:T(8,128)(2,1)}, bf16[768,...) custom-call(s32[16,23]{1,0:T(8,128)} %labels.3, s32[16]{0:T(128)} %flen.1, s32[16]{0:T(128)} %llen.3, ...), custom_call_target="tpu_custom_call" | custom-call | tf_op jit(solution)/shard_map/joint_backward/pallas_call | solution.py:614
  99.0 8.5 %finish.1 = (f32[1,16]{1,0:T(1,128)}, f32[1024,640]{1,0:T(8,128)}, f32[640,1024]{1,0:T(8,128)}, f32[1024,640]{1,0:T(8,128)}, f32[384,1024]{1,0:T(8,128)}, /*index=5*/bf16[384,1024]{1,0:T(8,128)(2,1)}) custom-call(f32[8,128]{1,0:T(8,128)} %get-tuple-element.26.loss, bf16[768,640]{1,0:T(8,128)(2,1)} %get-tuple-element.27.refs_0_, bf16[384,1024]{1,0:T(8,128)(2,1)} %bitcast.9, ...), custom_call_target="tpu_custom_call" | custom-call | tf_op jit(solution)/shard_map/finish/pallas_call | solution.py:690
